TPU v7x, 128 devices: a whole 4x4x4 slice. The times are simulated.
128 devices in a mesh: asset: 32 (over y, z, core), tm: 4 (over x).
Axes of the slice: x: 4, y: 4, z: 4, core: 2. Of those that a mesh axis runs over, the one named last changes fastest.
Arguments:
- values: float32 [4, 1024, 65536], P(None, 'tm', 'asset'), may hold values from -64 to 64
- listed_from: int32 [65536], P('asset'), may hold values from -1024 to 1023, as said below
- listed_until: int32 [65536], P('asset'), may hold values from -960 to 3070, as said below
Outputs:
- standardized: float32 [4, 1024, 65536], P(None, 'tm', 'asset')
Inputs may be any that keep to these rules, and one draw needn't show every extreme that they name: listed_until[a] - listed_from[a] is at least 64. listed_until[a] - listed_from[a] is at least 64.
All inputs are finite; a program needn't handle non-finite values.
Results may differ from a plain program's by a relative error of at most 0.00005.
Values sent between devices are 32-bit elements; how exact they have to be, the bound alone decides.
No kernel may reach another device: no remote copies, remote signals or barrier semaphores. Data moves between devices by JAX's collectives and lax.ppermute only.
A program may use at most 128 MiB of HBM per device.

v0:
```python
import jax
import jax.numpy as jnp
from jax import lax
from jax.sharding import PartitionSpec as P

WINDOW = 64


def passed_along(block, axis, distance):
    devices = range(lax.axis_size(axis))
    route = [(i - distance, i) for i in devices if i - distance in devices]
    return lax.ppermute(block, axis, route)


def sent_to_all(x, axis):
    copies = jnp.broadcast_to(x, (lax.axis_size(axis), *x.shape))
    return lax.all_to_all(copies, axis, split_axis=0, concat_axis=0, tiled=True)


def of_everyone(x, axis):
    everything = sent_to_all(x, axis)
    return jnp.sum(everything, axis=0)


def in_one(arrays, axis):
    line, at, finished = (jnp.concatenate([a.reshape(-1) for a in arrays]), 0, [])
    running = of_everyone(line, axis)
    for a in arrays:
        finished.append(running[at : at + a.size].reshape(a.shape))
        at += a.size
    return tuple(finished)


def listing(stamps, listed_from, listed_until):
    opened = listed_from[None, :]
    closed = listed_until[None, :]
    weight = ((stamps >= opened) & (stamps < closed)).astype(jnp.float32)
    window_low = jnp.maximum(jnp.maximum(stamps - (WINDOW - 1), opened), 0)
    window_high = jnp.minimum(stamps, closed - 1)
    counted = jnp.maximum(window_high - window_low + 1, 1)
    return (weight, counted.astype(jnp.float32))


def window_sums(masked):
    field_count, row_count, asset_count = masked.shape
    blocks = row_count // WINDOW
    current = masked.reshape(field_count, blocks, WINDOW, asset_count)
    offset = jnp.arange(WINDOW, dtype=jnp.int32)
    lower_band = (offset[None, :] <= offset[:, None]).astype(jnp.float32)
    upper_band = (offset[None, :] > offset[:, None]).astype(jnp.float32)
    highest = lax.Precision.HIGHEST
    within = jnp.einsum("ij,fbja->fbia", lower_band, current, precision=highest)
    tail_rows = passed_along(masked[:, row_count - WINDOW :], "tm", 1)
    carried = jnp.einsum("ij,fja->fia", upper_band, tail_rows, precision=highest)
    earlier = jnp.einsum("ij,fbja->fbia", upper_band, current[:, : blocks - 1], precision=highest)
    spread_in = jnp.concatenate([carried[:, None], earlier], axis=1)
    return (within + spread_in).reshape(field_count, row_count, asset_count)


def standardize(field_values, weight, count_part, count_total):
    local_sum = jnp.sum(field_values * weight[None], axis=2)
    local_sq = jnp.sum(weight[None] * field_values * field_values, axis=2)
    if count_total is None:
        count_total, totals, squares = in_one((count_part, local_sum, local_sq), "asset")
    else:
        totals, squares = in_one((local_sum, local_sq), "asset")
    count_floor = jnp.maximum(count_total, 1.0)[None, :]
    center = totals / count_floor
    spread = jnp.maximum(squares / count_floor - center * center, 0.0)
    deviate = (field_values - center[:, :, None]) * weight[None]
    return (deviate / jnp.sqrt(spread + 0.1)[:, :, None], count_total)


def per_device(values, listed_from, listed_until):
    field_count, row_count, asset_count = values.shape
    stamps = lax.axis_index("tm") * row_count + lax.broadcasted_iota(
        jnp.int32, (row_count, asset_count), 0
    )
    weight, counted = listing(stamps, listed_from, listed_until)
    masked = values * weight[None]
    rolling = window_sums(masked) / counted[None]
    count_part = jnp.sum(weight, axis=1)
    scored, count_total = standardize(rolling, weight, count_part, None)
    clipped = jnp.clip(scored, -3.0, 3.0)
    result_field, unused = standardize(clipped, weight, None, count_total)
    return result_field


def solution(mesh):
    in_specs = (P(None, "tm", "asset"), P("asset"), P("asset"))
    out_specs = P(None, "tm", "asset")
    return jax.shard_map(
        per_device, mesh=mesh, in_specs=in_specs, out_specs=out_specs, check_vma=False
    )
```

profile of v0, /device:TPU:1, one launch (start us, length us, event | category | flops | bytes accessed | tf_op | source)
XLA Modules:
  0.0 117.4 jit_solution(9558186845676015570)
XLA Ops:
  0.0 1.1 and_convert_fusion.1
  1.1 0.0 copy-start.1
  1.1 0.0 copy-start.2
  1.1 0.0 copy-start.3
  1.1 5.4 %broadcast_multiply_fusion = f32[4,256,2048]{2,1,0:T(8,128)S(1)} fusion(f32[4,256,2048]{2,1,0:T(8,128)} %param.3, f32[256,2048]{1,0:T(8,128)S(1)} %and_convert_fusion.1), kind=kLoop, calls=%fused_computation.17 | loop fusion | flops 2097152 | bytes 18874368 | tf_op jit(solution)/shard_map/mul | solution.py:80
  6.6 0.0 copy-done.1
  6.6 0.2 slice.72
  6.8 4.1 %collective-permute-start = (f32[4,64,2048]{2,1,0:T(8,128)S(1)}, f32[4,64,2048]{2,1,0:T(8,128)S(1)}, u32[]{:S(2)}, u32[]{:S(2)}) collective-permute-start(f32[4,64,2048]{2,1,0:T(8,128)S(1)} %slice.72), channel_id=1, source_target_pairs={{0,1},{1,2},{2,3},{4,5},{5,6},{6,7},{8,9},{9,10},{10,11},{12,13},{... | collective-permute-start | bytes 6291464 | tf_op jit(solution)/shard_map/ppermute | solution.py:12
  10.9 0.0 copy-done.2
  10.9 0.0 copy-done.3
  10.9 0.5 fusion.9
  11.4 0.4 and_convert_fusion
  11.8 0.8 maximum_convert_fusion
  12.6 0.0 copy-start
  12.6 6.3 %convolution_bitcast_fusion = f32[4,3,64,2048]{3,2,1,0:T(8,128)} fusion(f32[4,4,64,2048]{3,2,1,0:T(8,128)S(1)} %bitcast.43), kind=kOutput, calls=%fused_computation.18 | convolution fusion | flops 1207963648 | bytes 14680064 | tf_op jit(solution)/shard_map/ij,fbja->fbia/dot_general | solution.py:55
  18.9 36.1 %collective-permute-done = f32[4,64,2048]{2,1,0:T(8,128)S(1)} collective-permute-done((f32[4,64,2048]{2,1,0:T(8,128)S(1)}, f32[4,64,2048]{2,1,0:T(8,128)S(1)}, u32[]{:S(2)}, u32[]{:S(2)}) %collective-permute-start) | collective-permute-done | bytes 2097184 | tf_op jit(solution)/shard_map/ppermute | solution.py:12
  55.0 1.4 %convolution_bitcast_fusion.1 = f32[4,1,64,2048]{3,2,1,0:T(8,128)S(1)} fusion(f32[4,64,2048]{2,1,0:T(8,128)S(1)} %collective-permute-done), kind=kOutput, calls=%fused_computation.19 | convolution fusion | flops 402657280 | bytes 4194304 | tf_op jit(solution)/shard_map/ij,fja->fia/dot_general | solution.py:54
  56.4 0.0 copy-done
  56.4 12.8 %multiply_reduce_fusion.1 = (f32[4,4,64]{2,1,0:T(4,128)S(1)}, f32[4,4,64]{2,1,0:T(4,128)S(1)}, f32[4,4,64,2048]{3,2,1,0:T(8,128)}) fusion(f32[4,64,2048]{2,1,0:T(8,128)S(1)} %and_convert_fusion, f32[4,64,2048]{2,1,0:T(8,128)S(1)} %maximum_convert_fusion, f32[4,3,64,2048]{3,2,1,0:T(8,128)} %convolution_bitcast_fusion, ...), kind=kOutput, calls=%fused_computation.3 | convolution fusion | flops 1625294848 | bytes 29368320 | tf_op jit(solution)/shard_map/ij,fbja->fbia/dot_general | solution.py:52
  69.2 0.1 reshape.233
  69.2 0.1 reshape.234
  69.3 0.9 broadcast_in_dim.7
  70.2 9.6 %all-to-all-start = ((f32[32,1,2304]{2,1,0:T(1,128)}), f32[32,1,2304]{2,1,0:T(1,128)S(1)}, u32[]{:S(2)}, u32[]{:S(2)}) async-start(f32[32,1,2304]{2,1,0:T(1,128)} %broadcast_in_dim.7), calls=%async_computation | async-start | bytes 589824 | tf_op jit(solution)/shard_map/all_to_all | solution.py:17
  79.8 9.3 %all-to-all-done = f32[32,1,2304]{2,1,0:T(1,128)S(1)} async-done(((f32[32,1,2304]{2,1,0:T(1,128)}), f32[32,1,2304]{2,1,0:T(1,128)S(1)}, u32[]{:S(2)}, u32[]{:S(2)}) %all-to-all-start) | async-done | bytes 294944 | tf_op jit(solution)/shard_map/all_to_all | solution.py:17
  89.1 0.2 reduce_sum.66
  89.4 0.1 div.75
  89.4 0.1 sub.59
  89.5 6.6 %multiply_reduce_fusion = (f32[4,4,64]{2,1,0:T(4,128)S(1)}, f32[4,4,64]{2,1,0:T(4,128)S(1)}) fusion(f32[4,64,2048]{2,1,0:T(8,128)S(1)} %and_convert_fusion, f32[4,4,64]{2,1,0:T(4,128)S(1)} %div.75, f32[4,4,64]{2,1,0:T(4,128)S(1)} %sub.59, f32[4,4,64,2048]{3,2,1,0:T(8,128)} %get-tuple-element.17, f32[4,64,2048]{2,1,0:T(8,128)} %copy-done), kind=kLoop, calls=%fused_computation.1 | loop fusion | flops 18872320 | bytes 12599296 | tf_op jit(solution)/shard_map/reduce_sum | solution.py:61
  96.1 0.1 reshape.235
  96.2 0.1 reshape.236
  96.2 0.8 broadcast_in_dim.8
  97.1 3.7 %all-to-all-start.1 = ((f32[32,1,2048]{2,1,0:T(1,128)}), f32[32,1,2048]{2,1,0:T(1,128)S(1)}, u32[]{:S(2)}, u32[]{:S(2)}) async-start(f32[32,1,2048]{2,1,0:T(1,128)} %broadcast_in_dim.8), calls=%async_computation.1 | async-start | bytes 524288 | tf_op jit(solution)/shard_map/all_to_all | solution.py:17
  100.8 0.8 maximum_convert_fusion.1
  101.6 8.2 %all-to-all-done.1 = f32[32,1,2048]{2,1,0:T(1,128)S(1)} async-done(((f32[32,1,2048]{2,1,0:T(1,128)}), f32[32,1,2048]{2,1,0:T(1,128)S(1)}, u32[]{:S(2)}, u32[]{:S(2)}) %all-to-all-start.1) | async-done | bytes 262176 | tf_op jit(solution)/shard_map/all_to_all | solution.py:17
  109.8 0.2 reduce_sum.69
  110.1 7.3 %fusion.8 = f32[4,256,2048]{2,1,0:T(8,128)} fusion(f32[4,4,64,2048]{3,2,1,0:T(8,128)} %get-tuple-element.17, f32[4,256]{1,0:T(4,128)S(1)} %get-tuple-element.14, f32[4,256]{1,0:T(4,128)S(1)} %get-tuple-element.13, f32[4,256]{1,0:T(4,128)S(1)} %get-tuple-element.16, f32[4,256]{1,0:T(4,128)S(1)} %get-tuple-element.15, ...), kind=kLoop, calls=%fused_computation.14 | loop fusion | flops 16777216 | bytes 20987904 | tf_op jit(solution)/shard_map/div | solution.py:71
  (15 shorter events, 0.1 us)
Async XLA Ops:
  1.1 5.5 %copy-start.1 = (f32[256,2048]{1,0:T(8,128)}, f32[256,2048]{1,0:T(8,128)S(1)}, u32[]{:S(2)}) copy-start(f32[256,2048]{1,0:T(8,128)S(1)} %and_convert_fusion.1) | copy-start | bytes 6291460
  1.1 9.8 %copy-start.2 = (s32[2048]{0:T(1024)S(1)}, s32[2048]{0:T(1024)}, u32[]{:S(2)}) copy-start(s32[2048]{0:T(1024)} %param.4) | copy-start | bytes 24580
  1.1 9.8 %copy-start.3 = (s32[2048]{0:T(1024)S(1)}, s32[2048]{0:T(1024)}, u32[]{:S(2)}) copy-start(s32[2048]{0:T(1024)} %param.5) | copy-start | bytes 24580
  6.8 48.2 %collective-permute-start = (f32[4,64,2048]{2,1,0:T(8,128)S(1)}, f32[4,64,2048]{2,1,0:T(8,128)S(1)}, u32[]{:S(2)}, u32[]{:S(2)}) collective-permute-start(f32[4,64,2048]{2,1,0:T(8,128)S(1)} %slice.72), channel_id=1, source_target_pairs={{0,1},{1,2},{2,3},{4,5},{5,6},{6,7},{8,9},{9,10},{10,11},{12,13},{... | collective-permute-start | bytes 6291464 | tf_op jit(solution)/shard_map/ppermute | solution.py:12
  12.6 43.8 %copy-start = (f32[4,64,2048]{2,1,0:T(8,128)}, f32[4,64,2048]{2,1,0:T(8,128)S(1)}, u32[]{:S(2)}) copy-start(f32[4,64,2048]{2,1,0:T(8,128)S(1)} %maximum_convert_fusion) | copy-start | bytes 6291460
  70.2 18.9 %all-to-all-start = ((f32[32,1,2304]{2,1,0:T(1,128)}), f32[32,1,2304]{2,1,0:T(1,128)S(1)}, u32[]{:S(2)}, u32[]{:S(2)}) async-start(f32[32,1,2304]{2,1,0:T(1,128)} %broadcast_in_dim.7), calls=%async_computation | async-start | bytes 589824 | tf_op jit(solution)/shard_map/all_to_all | solution.py:17
  97.1 12.8 %all-to-all-start.1 = ((f32[32,1,2048]{2,1,0:T(1,128)}), f32[32,1,2048]{2,1,0:T(1,128)S(1)}, u32[]{:S(2)}, u32[]{:S(2)}) async-start(f32[32,1,2048]{2,1,0:T(1,128)} %broadcast_in_dim.8), calls=%async_computation.1 | async-start | bytes 524288 | tf_op jit(solution)/shard_map/all_to_all | solution.py:17
where the time goes:
time: 118 us; the launch traced here: 117 us
  waiting for transfers between devices  53.6 us (45%)
  other arithmetic  23.3 us (20%)
  matrix products  20.4 us (17%)
  starting transfers between devices  17.4 us (15%)
  local copies, waits for them, and re-layouts  2.47 us (2%)
    ppermute x1, waiting for transfers between devices, passed_along(): return lax.ppermute(block, axis, route)  36.1 us
    all_to_all x2, waiting for transfers between devices, sent_to_all(): return lax.all_to_all(copies, axis, split_axis=0, concat_axis=0, tiled=True)  17.5 us
    all_to_all x2, starting transfers between devices, sent_to_all(): return lax.all_to_all(copies, axis, split_axis=0, concat_axis=0, tiled=True)  13.3 us
    dot_general x1, matrix products, window_sums(): within = jnp.einsum('ij,fbja->fbia', lower_band, current, precision=highest)  12.8 us
    div x1, other arithmetic, standardize(): return (deviate / jnp.sqrt(spread + 0.1)[:, :, None], count_total)  7.32 us
    reduce_sum x1, other arithmetic, standardize(): local_sum = jnp.sum(field_values * weight[None], axis=2)  6.55 us
    dot_general x1, matrix products, window_sums(): jnp.einsum('ij,fbja->fbia', upper_band, current[:, :blocks - 1], precisio...  6.31 us
    mul x1, other arithmetic, per_device(): masked = values * weight[None]  5.44 us
  transfers between devices with their start and end apart: 3, of which 3 were waited for; matrix products, arithmetic and copies ran while one was open for 8% of the time, Pallas kernels for 0%

commit v1 on v0

v1 whole, which is shorter than its diff:
```python
import functools

import jax
import jax.numpy as jnp
from jax import lax
from jax.experimental import pallas as pl
from jax.experimental.pallas import tpu as pltpu
from jax.sharding import PartitionSpec as P

WINDOW = 64
EPS = 0.1
LIMIT = 3.0
GROUP = 8
LANE = 128
LATE = 32
LATE_GROUPS = LATE // GROUP
SKIP_GROUPS = WINDOW // GROUP
VMEM = pl.BlockSpec(memory_space=pltpu.VMEM)
SMEM = pl.BlockSpec(memory_space=pltpu.SMEM)
ANY = pl.BlockSpec(memory_space=pl.ANY)
MIB = 1 << 20


def rows_of(g):
    return pl.ds(g * GROUP, GROUP)


def sublanes(width):
    return lax.broadcasted_iota(jnp.int32, (GROUP, width), 0)


def lanes_iota():
    return lax.broadcasted_iota(jnp.int32, (GROUP, LANE), 1)


def folded(x):
    total = x[:, :LANE]
    for at in range(LANE, x.shape[1], LANE):
        total = total + x[:, at : at + LANE]
    return total


def total_of(x):
    return jnp.sum(x, axis=1, keepdims=True)


def column(tile, lane, width):
    return jnp.broadcast_to(tile[:, lane : lane + 1], (GROUP, width))


def clipped_score(x, center, scale):
    return jnp.minimum(jnp.maximum((x - center) * scale, -LIMIT), LIMIT)


def moments(total, square, present):
    center = total / present
    spread = jnp.maximum(square / present - center * center, 0.0)
    return center, 1.0 / jnp.sqrt(spread + EPS)


def summed(gathered):
    total = gathered[0]
    for d in range(1, gathered.shape[0]):
        total = total + gathered[d]
    return total


def prefix_groups(groups, width):
    sub = sublanes(width)
    carried, out = None, []
    for x in groups:
        for s in (1, 2, 4):
            x = x + jnp.where(sub < s, 0.0, pltpu.roll(x, s, 0))
        if carried is not None:
            x = x + carried
        carried = jnp.broadcast_to(x[GROUP - 1 :, :], (GROUP, width))
        out.append(x)
    return out, carried


def first_pass(times, x_hbm, from_ref, until_ref, buf, inverse, pay, xs, sums, counts, sems):
    fields, rows, assets = x_hbm.shape
    own_groups = rows // GROUP
    groups = own_groups + LATE_GROUPS
    main = own_groups - SKIP_GROUPS
    chunks, _, _, width = xs.shape
    base, base_next = times[0], times[1]

    def fetch(c):
        lanes = pl.ds(pl.multiple_of(c * width, width), width)
        return pltpu.make_async_copy(x_hbm.at[:, :, lanes], xs.at[c], sems.at[c])

    for c in range(chunks):
        fetch(c).start()
    sums[...] = jnp.zeros_like(sums)
    counts[...] = jnp.zeros_like(counts)
    sub = sublanes(width)

    def chunk(c, carry):
        lanes = pl.ds(pl.multiple_of(c * width, width), width)
        opened = jnp.maximum(from_ref[:, lanes], 0)
        closed = until_ref[:, lanes]
        age = sub - opened
        left = closed - sub
        for g in range(groups):
            at = base + g * GROUP if g < own_groups else base_next + (g - own_groups) * GROUP
            seen = age + at
            listed = (seen >= 0) & (left > at)
            counted = jnp.clip(seen + 1, 1, WINDOW).astype(jnp.float32)
            inverse[rows_of(g), lanes] = jnp.where(listed, 1.0 / counted, 0.0)
            if g >= SKIP_GROUPS - LATE_GROUPS:
                which = g - (SKIP_GROUPS - LATE_GROUPS)
                counts[which] += folded(jnp.where(listed, 1.0, 0.0))
        fetch(c).wait()
        start = base + age

        def one_field(f, carry):
            last1 = last2 = last4 = last8 = None
            last16, last32 = [], []
            for g in range(groups):
                if g < own_groups:
                    x = jnp.where(start >= -g * GROUP, xs[c, f, rows_of(g), :], 0.0)
                else:
                    x = jnp.zeros((GROUP, width), jnp.float32)
                r = pltpu.roll(x, 1, 0)
                x = x + jnp.where(sub < 1, 0.0 if last1 is None else last1, r)
                last1 = r
                r = pltpu.roll(x, 2, 0)
                x = x + jnp.where(sub < 2, 0.0 if last2 is None else last2, r)
                last2 = r
                r = pltpu.roll(x, 4, 0)
                x = x + jnp.where(sub < 4, 0.0 if last4 is None else last4, r)
                last4 = r
                x16 = x if last8 is None else x + last8
                last8 = x
                x32 = x16 if len(last16) < 2 else x16 + last16[-2]
                last16 = last16[-1:] + [x16]
                x64 = x32 if len(last32) < 4 else x32 + last32[-4]
                last32 = last32[-3:] + [x32]
                if SKIP_GROUPS <= g < own_groups:
                    x64 = x64 * inverse[rows_of(g), lanes]
                    sums[0, f, g - SKIP_GROUPS] += folded(x64)
                    sums[1, f, g - SKIP_GROUPS] += folded(x64 * x64)
                buf[f, rows_of(g), lanes] = x64
            return carry

        lax.fori_loop(0, fields, one_field, 0)
        return carry

    lax.fori_loop(0, chunks, chunk, 0)
    lane = lanes_iota()
    tiles = [jnp.zeros((GROUP, LANE), jnp.float32) for _ in range(2)]
    for stat in range(2):
        for f in range(fields):
            for g in range(main):
                tiles[stat] = jnp.where(lane == f * main + g, total_of(sums[stat, f, g]), tiles[stat])
    first = fields * main
    for g in range(main):
        tiles[0] = jnp.where(lane == first + g, total_of(counts[LATE_GROUPS + g]), tiles[0])
    for side in range(2):
        for g in range(LATE_GROUPS):
            spot = lane - (first + side * fields * LATE_GROUPS)
            here = (spot >= 0) & (spot < fields * LATE_GROUPS) & (lax.rem(spot, LATE_GROUPS) == g)
            at = g if side == 0 else LATE_GROUPS + main + g
            tiles[1] = jnp.where(here, total_of(counts[at]), tiles[1])
    for d in range(pay.shape[0]):
        pay[d, :GROUP, :] = tiles[0]
        pay[d, GROUP:, :] = tiles[1]


def second_pass(gathered, buf, inverse, stats, part):
    fields, _, assets = buf.shape
    main = (inverse.shape[0] - LATE) // GROUP - SKIP_GROUPS
    first = fields * main
    total = summed(gathered)
    t0, t1 = total[:GROUP], total[GROUP:]
    lane = lanes_iota()
    present = t1
    for f in range(fields):
        moved = pltpu.roll(t0, (f * main - first) % LANE, 1)
        present = jnp.where((lane >= f * main) & (lane < (f + 1) * main), moved, present)
    present = jnp.maximum(present, 1.0)
    center, scale = moments(t0, t1, present)
    stats[0], stats[1], stats[2] = center, scale, present
    width = 4 * LANE
    tiles = [jnp.zeros((GROUP, LANE), jnp.float32) for _ in range(2)]
    for g in range(main):
        rows = rows_of(g + SKIP_GROUPS)
        cs = [column(center, f * main + g, width) for f in range(fields)]
        ss = [column(scale, f * main + g, width) for f in range(fields)]

        def tile(i, acc):
            lanes = pl.ds(pl.multiple_of(i * width, width), width)
            listed = inverse[rows, lanes] > 0.0
            acc = list(acc)
            for f in range(fields):
                z = clipped_score(buf[f, rows, lanes], cs[f], ss[f])
                z = jnp.where(listed, z, 0.0)
                acc[f] = acc[f] + folded(z)
                acc[fields + f] = acc[fields + f] + folded(z * z)
            return tuple(acc)

        zero = jnp.zeros((GROUP, LANE), jnp.float32)
        acc = lax.fori_loop(0, assets // width, tile, (zero,) * (2 * fields))
        for f in range(fields):
            for stat in range(2):
                tiles[stat] = jnp.where(
                    lane == f * main + g, total_of(acc[stat * fields + f]), tiles[stat]
                )
    part[:GROUP, :] = tiles[0]
    part[GROUP:, :] = tiles[1]


def late_first_pass(times, buf, tail, head, from_ref, inverse, part, late, whole, pay):
    fields, _, assets = buf.shape
    rows = inverse.shape[0] - LATE
    base, base_next = times[0], times[1]
    follows = jnp.where(base_next > 0, 1.0, 0.0)
    width = LANE
    sub = sublanes(width)
    lane = lanes_iota()
    first = LANE - 2 * fields * LATE_GROUPS
    tiles = [part[:GROUP, :], part[GROUP:, :]]
    for f in range(fields):

        def tile(i, acc):
            lanes = pl.ds(pl.multiple_of(i * width, width), width)
            age = sub - jnp.maximum(from_ref[:, lanes], 0)
            acc = list(acc)
            for side, ref, at in ((0, tail, base - LATE), (1, head, base_next)):
                start = age + at
                masked = [
                    jnp.where(start >= -g * GROUP, ref[f, rows_of(g), lanes], 0.0)
                    for g in range(LATE_GROUPS)
                ]
                running, last = prefix_groups(masked, width)
                if side == 0:
                    whole[f, :, lanes] = last
                for g in range(LATE_GROUPS):
                    if side == 0:
                        where = rows_of(LATE_GROUPS + g)
                        r = buf[f, where, lanes] + (last - running[g])
                    else:
                        where = rows_of(rows // GROUP + g)
                        r = buf[f, where, lanes] * follows + running[g]
                    r = r * inverse[where, lanes]
                    late[f, rows_of(side * LATE_GROUPS + g), lanes] = r
                    k = side * LATE_GROUPS + g
                    acc[k] = acc[k] + r
                    acc[2 * LATE_GROUPS + k] = acc[2 * LATE_GROUPS + k] + r * r
            return tuple(acc)

        zero = jnp.zeros((GROUP, LANE), jnp.float32)
        acc = lax.fori_loop(0, assets // width, tile, (zero,) * (4 * LATE_GROUPS))
        for side in range(2):
            for g in range(LATE_GROUPS):
                spot = first + (side * fields + f) * LATE_GROUPS + g
                for stat in range(2):
                    value = total_of(acc[(stat * 2 + side) * LATE_GROUPS + g])
                    tiles[stat] = jnp.where(lane == spot, value, tiles[stat])
    for d in range(pay.shape[0]):
        pay[d, :GROUP, :] = tiles[0]
        pay[d, GROUP:, :] = tiles[1]


def late_second_pass(gathered, stats, late, inverse, level, pay):
    fields, _, assets = late.shape
    rows = inverse.shape[0] - LATE
    total = summed(gathered)
    center, scale = moments(total[:GROUP], total[GROUP:], stats[2])
    level[0], level[1] = center, scale
    width = 4 * LANE
    first = LANE - 2 * fields * LATE_GROUPS
    lane = lanes_iota()
    out = jnp.zeros((GROUP, LANE), jnp.float32)
    for side in range(2):
        for g in range(LATE_GROUPS):
            spots = [first + (side * fields + f) * LATE_GROUPS + g for f in range(fields)]
            cs = [column(center, spot, width) for spot in spots]
            ss = [column(scale, spot, width) for spot in spots]
            where = rows_of(LATE_GROUPS + g if side == 0 else rows // GROUP + g)
            mine = rows_of(side * LATE_GROUPS + g)

            def tile(i, acc):
                lanes = pl.ds(pl.multiple_of(i * width, width), width)
                listed = inverse[where, lanes] > 0.0
                acc = list(acc)
                for f in range(fields):
                    z = clipped_score(late[f, mine, lanes], cs[f], ss[f])
                    z = jnp.where(listed, z, 0.0)
                    acc[f] = acc[f] + folded(z)
                    acc[fields + f] = acc[fields + f] + folded(z * z)
                return tuple(acc)

            zero = jnp.zeros((GROUP, LANE), jnp.float32)
            acc = lax.fori_loop(0, assets // width, tile, (zero,) * (2 * fields))
            back = LANE - first
            for f in range(fields):
                out = jnp.where(lane == spots[f], total_of(acc[f]), out)
                out = jnp.where(lane == spots[f] - back, total_of(acc[fields + f]), out)
    for d in range(pay.shape[0]):
        pay[d] = out


def final_rows(f, where, source, mine, inverse, stage, put, cols, assets):
    width = 4 * LANE
    c1, s1, c2, s2 = cols

    def tile(i, carry):
        lanes = pl.ds(pl.multiple_of(i * width, width), width)
        z = clipped_score(source[f, mine, lanes], c1, s1)
        z = (z - c2) * s2
        stage[f, put, lanes] = jnp.where(inverse[where, lanes] > 0.0, z, 0.0)
        return carry

    lax.fori_loop(0, assets // width, tile, 0)


def main_final_pass(buf, inverse, stats, level, out, stage, sems):
    fields, rows, assets = out.shape
    main = rows // GROUP - SKIP_GROUPS
    width = 4 * LANE
    c1, s1, c2, s2 = stats[0], stats[1], level[0], level[1]
    copies = []
    for f in range(fields):
        for g in range(main):
            spot = f * main + g
            where = rows_of(g + SKIP_GROUPS)
            cols = [column(t, spot, width) for t in (c1, s1, c2, s2)]
            final_rows(f, where, buf, where, inverse, stage, rows_of(g), cols, assets)
        copy = pltpu.make_async_copy(
            stage.at[f], out.at[f, pl.ds(WINDOW, rows - WINDOW), :], sems.at[f]
        )
        copy.start()
        copies.append(copy)
    for copy in copies:
        copy.wait()


def send_pass(gathered, stats, level, level4, pay):
    total = summed(gathered)
    back = 32
    square = pltpu.roll(total, back, 1)
    center, scale = moments(total, square, stats[2])
    level4[0], level4[1] = center, scale
    lane = lanes_iota()
    out = jnp.zeros((GROUP, LANE), jnp.float32)
    for i, t in enumerate((level[0], level[1], center, scale)):
        moved = pltpu.roll(t, 16 * (i + 1), 1)
        out = jnp.where((lane >= 16 * i) & (lane < 16 * (i + 1)), moved, out)
    pay[...] = out


def late_final_pass(late, inverse, level, level4, prior, out, stage, sems):
    fields, _, assets = late.shape
    width = 4 * LANE
    first = LANE - 2 * fields * LATE_GROUPS
    copies = []
    for f in range(fields):
        for g in range(LATE_GROUPS):
            spot = first + f * LATE_GROUPS + g
            tiles = (level[0], level[1], level4[0], level4[1])
            cols = [column(t, spot, width) for t in tiles]
            where = rows_of(LATE_GROUPS + g)
            final_rows(f, where, late, rows_of(g), inverse, stage, rows_of(g), cols, assets)
        copy = pltpu.make_async_copy(stage.at[f], out.at[f, pl.ds(LATE, LATE), :], sems.at[f])
        copy.start()
        copies.append(copy)
    for copy in copies:
        copy.wait()


def head_final_pass(times, buf, tail, whole, from_ref, inverse, sent, prior, out, stage, sems):
    fields, _, assets = buf.shape
    base = times[0]
    width = 2 * LANE
    sub = sublanes(width)
    levels = sent[...]
    copies = []
    for f in range(fields):
        cols = [
            [column(levels, 16 * i + f * LATE_GROUPS + g, width) for i in range(4)]
            for g in range(LATE_GROUPS)
        ]

        def tile(i, carry):
            lanes = pl.ds(pl.multiple_of(i * width, width), width)
            start = sub - jnp.maximum(from_ref[:, lanes], 0) + (base - WINDOW)
            masked = [
                jnp.where(start >= -g * GROUP, tail[f, rows_of(g), lanes], 0.0)
                for g in range(LATE_GROUPS)
            ]
            running, last = prefix_groups(masked, width)
            last = last + whole[f, :, lanes]
            for g in range(LATE_GROUPS):
                c1, s1, c2, s2 = cols[g]
                weight = inverse[rows_of(g), lanes]
                r = (buf[f, rows_of(g), lanes] + (last - running[g])) * weight
                z = (clipped_score(r, c1, s1) - c2) * s2
                stage[f, rows_of(g), lanes] = jnp.where(weight > 0.0, z, 0.0)
            return carry

        lax.fori_loop(0, assets // width, tile, 0)
        copy = pltpu.make_async_copy(stage.at[f], out.at[f, pl.ds(0, LATE), :], sems.at[f])
        copy.start()
        copies.append(copy)
    for copy in copies:
        copy.wait()


def shape(*dims):
    return jax.ShapeDtypeStruct(dims, jnp.float32)


def call(body, name, ins, outs, out_specs, scratch=(), limit=8, flops=0, aliases=None):
    return pl.pallas_call(
        body,
        name=name,
        out_shape=outs,
        in_specs=ins,
        out_specs=out_specs,
        scratch_shapes=list(scratch),
        input_output_aliases=aliases or {},
        compiler_params=pltpu.CompilerParams(vmem_limit_bytes=limit * MIB),
        cost_estimate=pl.CostEstimate(flops=flops, bytes_accessed=0, transcendentals=0),
    )


def per_device(values, listed_from, listed_until):
    fields, rows, assets = values.shape
    n = lax.axis_size("asset")
    blocks = lax.axis_size("tm")
    block = lax.axis_index("tm")
    forward = [(i, i + 1) for i in range(blocks - 1)]
    ring = [(i, (i + 1) % blocks) for i in range(blocks)]
    back = [((i + 1) % blocks, i) for i in range(blocks)]
    tail_near = lax.ppermute(values[:, rows - LATE :], "tm", forward)
    head = lax.ppermute(values[:, :LATE], "tm", back)
    tail_far = lax.ppermute(values[:, rows - WINDOW : rows - LATE], "tm", forward)
    times = jnp.stack([block * rows, lax.rem(block + 1, blocks) * rows]).astype(jnp.int32)
    opened, closed = listed_from.reshape(1, assets), listed_until.reshape(1, assets)
    main = rows // GROUP - SKIP_GROUPS
    width = 2 * LANE
    chunks = assets // width
    tile = shape(GROUP, LANE)
    pair = shape(2, GROUP, LANE)
    exchange = functools.partial(
        lax.all_to_all, axis_name="asset", split_axis=0, concat_axis=0, tiled=True
    )
    work = fields * rows * assets

    buf, inverse, pay = call(
        first_pass, "first_pass", [SMEM, ANY, VMEM, VMEM],
        (shape(fields, rows + LATE, assets), shape(rows + LATE, assets), shape(n, 2 * GROUP, LANE)),
        (VMEM, VMEM, VMEM),
        [
            pltpu.VMEM((chunks, fields, rows, width), jnp.float32),
            pltpu.VMEM((2, fields, main, GROUP, LANE), jnp.float32),
            pltpu.VMEM((main + 2 * LATE_GROUPS, GROUP, LANE), jnp.float32),
            pltpu.SemaphoreType.DMA((chunks,)),
        ],
        limit=26, flops=20 * work,
    )(times, values, opened, closed)
    gathered = exchange(pay)
    stats, part = call(
        second_pass, "second_pass", [VMEM] * 3,
        (shape(3, GROUP, LANE), shape(2 * GROUP, LANE)), (VMEM, VMEM), limit=16, flops=10 * work,
    )(gathered, buf, inverse)
    late, whole, pay = call(
        late_first_pass, "late_first_pass", [SMEM] + [VMEM] * 6,
        (shape(fields, 2 * LATE, assets), shape(fields, GROUP, assets), shape(n, 2 * GROUP, LANE)),
        (VMEM, VMEM, VMEM), limit=20, flops=5 * work,
    )(times, buf, tail_near, head, opened, inverse, part)
    gathered = exchange(pay)
    level, pay = call(
        late_second_pass, "late_second_pass", [VMEM] * 4,
        (pair, shape(n, GROUP, LANE)), (VMEM, VMEM), limit=16, flops=3 * work,
    )(gathered, stats, late, inverse)
    gathered = exchange(pay)
    out = call(
        main_final_pass, "main_final_pass", [VMEM] * 4,
        shape(fields, rows, assets), ANY,
        [
            pltpu.VMEM((fields, rows - WINDOW, assets), jnp.float32),
            pltpu.SemaphoreType.DMA((fields,)),
        ],
        limit=20, flops=10 * work,
    )(buf, inverse, stats, level)
    level4, pay = call(
        send_pass, "send_pass", [VMEM] * 3, (pair, tile), (VMEM, VMEM), flops=work // 100,
    )(gathered, stats, level)
    sent = lax.ppermute(pay, "tm", ring)
    stage = [
        pltpu.VMEM((fields, LATE, assets), jnp.float32),
        pltpu.SemaphoreType.DMA((fields,)),
    ]
    out = call(
        late_final_pass, "late_final_pass", [VMEM] * 4 + [ANY],
        shape(fields, rows, assets), ANY, stage, limit=16, flops=2 * work, aliases={4: 0},
    )(late, inverse, level, level4, out)
    return call(
        head_final_pass, "head_final_pass", [SMEM] + [VMEM] * 6 + [ANY],
        shape(fields, rows, assets), ANY, stage, limit=16, flops=2 * work, aliases={7: 0},
    )(times, buf, tail_far, whole, opened, inverse, sent, out)


def solution(mesh):
    in_specs = (P(None, "tm", "asset"), P("asset"), P("asset"))
    out_specs = P(None, "tm", "asset")
    return jax.shard_map(
        per_device, mesh=mesh, in_specs=in_specs, out_specs=out_specs, check_vma=False
    )
```

time: 118 us -> 93 us (0.79)
  waiting for transfers between devices: 53.6 us -> 0.01 us
  blocking collectives: 0 us -> 42 us
  Pallas kernels: 0 us -> 33.5 us
  other arithmetic: 23.3 us -> 0.08 us
  matrix products: 20.4 us -> 0 us
  starting transfers between devices: 17.4 us -> 8.55 us
  local copies, waits for them, and re-layouts: 2.47 us -> 8.43 us
    all_to_all x0 -> x3, blocking collectives: none -> 42 us  [per_device(): gathered = exchange(pay)]
    ppermute x1 -> x4, waiting for transfers between devices: 36.1 us -> 0.01 us  [the longest x1 0.01 us: per_device(): sent = lax.ppermute(pay, 'tm', ring)]
    pallas_call x0 -> x8, Pallas kernels: none -> 33.5 us  [the longest x1 10.1 us: per_device(): call(main_final_pass, 'main_final_pass', [VMEM] * 4, shape(fields, rows,...]
    dot_general x3 -> x0, matrix products: 20.4 us -> none  [the longest x1 12.8 us: window_sums(): within = jnp.einsum('ij,fbja->fbia', lower_band, current, precision=highest)]
    all_to_all x2 -> x0, waiting for transfers between devices: 17.5 us -> none  [sent_to_all(): return lax.all_to_all(copies, axis, split_axis=0, concat_axis=0, tiled=True)]
    all_to_all x2 -> x0, starting transfers between devices: 13.3 us -> none  [sent_to_all(): return lax.all_to_all(copies, axis, split_axis=0, concat_axis=0, tiled=True)]
    reduce_sum x4 -> x0, other arithmetic: 7.38 us -> none  [the longest x1 6.55 us: standardize(): local_sum = jnp.sum(field_values * weight[None], axis=2)]
    div x3 -> x0, other arithmetic: 7.35 us -> none  [the longest x1 7.32 us: standardize(): return (deviate / jnp.sqrt(spread + 0.1)[:, :, None], count_total)]
  transfers between devices with their start and end apart: 3 -> 4, of which waited for: 3 -> 0; matrix products, arithmetic and copies ran while one was open for 8% -> 0% of each run, Pallas kernels for 0% -> 33%
where the time goes in v1:
time: 93 us; the launch traced here: 92.6 us
  blocking collectives  42 us (45%)
  Pallas kernels  33.5 us (36%)
  starting transfers between devices  8.55 us (9%)
  local copies, waits for them, and re-layouts  8.43 us (9%)
    all_to_all x3, blocking collectives, per_device(): gathered = exchange(pay)  42 us
    pallas_call x1, Pallas kernels, per_device(): call(main_final_pass, 'main_final_pass', [VMEM] * 4, shape(fields, rows,...  10.1 us
    pallas_call x1, Pallas kernels, per_device(): call(first_pass, 'first_pass', [SMEM, ANY, VMEM, VMEM], (shape(fields, ro...  8.21 us
    pallas_call x1, Pallas kernels, per_device(): call(second_pass, 'second_pass', [VMEM] * 3, (shape(3, GROUP, LANE), shap...  5.29 us
    unnamed x8, local copies, waits for them, and re-layouts  4.78 us
    slice x1, local copies, waits for them, and re-layouts, per_device(): head = lax.ppermute(values[:, :LATE], 'tm', back)  3.65 us
    ppermute x1, starting transfers between devices, per_device(): head = lax.ppermute(values[:, :LATE], 'tm', back)  3.3 us
    pallas_call x1, Pallas kernels, per_device(): call(late_first_pass, 'late_first_pass', [SMEM] + [VMEM] * 6, (shape(fiel...  2.95 us
  transfers between devices with their start and end apart: 4, of which 0 were waited for; matrix products, arithmetic and copies ran while one was open for 0% of the time, Pallas kernels for 33%

profile of v1, /device:TPU:1, one launch (start us, length us, event | category | flops | bytes accessed | tf_op | source)
XLA Modules:
  0.0 92.6 jit_solution(4420719389911450246)
XLA Ops:
  0.0 3.6 %fusion = (f32[4,32,2048]{2,1,0:T(8,128)}, f32[4,32,2048]{2,1,0:T(8,128)}, f32[4,32,2048]{2,1,0:T(8,128)}) fusion(f32[4,256,2048]{2,1,0:T(8,128)} %x_hbm.1), kind=kLoop, calls=%fused_computation.1 | loop fusion | bytes 6291456 | tf_op jit(solution)/shard_map/slice | solution.py:438
  3.7 3.3 %collective-permute-start.2 = (f32[4,32,2048]{2,1,0:T(8,128)}, f32[4,32,2048]{2,1,0:T(8,128)S(1)}, u32[]{:S(2)}, u32[]{:S(2)}) collective-permute-start(f32[4,32,2048]{2,1,0:T(8,128)} %get-tuple-element.29), channel_id=1, source_target_pairs={{1,0},{2,1},{3,2},{0,3},{5,4},{6,5},{7,6},{4,7},{9,8},{10,9},{11,1... | collective-permute-start | bytes 3145736 | tf_op jit(solution)/shard_map/ppermute | solution.py:438
  6.9 1.3 %collective-permute-start.1 = (f32[4,32,2048]{2,1,0:T(8,128)}, f32[4,32,2048]{2,1,0:T(8,128)S(1)}, u32[]{:S(2)}, u32[]{:S(2)}) collective-permute-start(f32[4,32,2048]{2,1,0:T(8,128)} %get-tuple-element.31), channel_id=1, source_target_pairs={{0,1},{1,2},{2,3},{4,5},{5,6},{6,7},{8,9},{9,10},{10,11},{12,13},{... | collective-permute-start | bytes 3145736 | tf_op jit(solution)/shard_map/ppermute | solution.py:437
  8.3 2.7 %collective-permute-start = (f32[4,32,2048]{2,1,0:T(8,128)}, f32[4,32,2048]{2,1,0:T(8,128)S(1)}, u32[]{:S(2)}, u32[]{:S(2)}) collective-permute-start(f32[4,32,2048]{2,1,0:T(8,128)} %get-tuple-element.30), channel_id=1, source_target_pairs={{0,1},{1,2},{2,3},{4,5},{5,6},{6,7},{8,9},{9,10},{10,11},{12,13},{... | collective-permute-start | bytes 3145736 | tf_op jit(solution)/shard_map/ppermute | solution.py:439
  11.0 0.1 pad_add_fusion.times
  11.1 0.0 copy-start
  11.1 3.4 %copy-done = f32[4,256,2048]{2,1,0:T(8,128)S(1)} copy-done((f32[4,256,2048]{2,1,0:T(8,128)S(1)}, f32[4,256,2048]{2,1,0:T(8,128)}, u32[]{:S(2)}) %copy-start) | copy-done | bytes 8388632
  14.5 0.0 copy-start.1
  14.5 0.7 copy-done.1
  15.2 0.0 copy-start.3
  15.2 0.7 copy-done.3
  15.9 8.2 %first_pass.1 = (f32[4,288,2048]{2,1,0:T(8,128)S(1)}, f32[288,2048]{1,0:T(8,128)S(1)}, f32[32,16,128]{2,1,0:T(8,128)S(1)}) custom-call(s32[2]{0:T(128)S(1)} %pad_add_fusion.times, f32[4,256,2048]{2,1,0:T(8,128)S(1)} %copy-done, s32[1,2048]{1,0:T(1,128)S(1)} %bitcast.4, s32[1,2048]{1,0:T(1,128)S(1)} %bitcast.7), custom_call_target="tpu_custom_call" | custom-call | flops 41943040 | tf_op jit(solution)/shard_map/first_pass/pallas_call | solution.py:452
  24.1 0.0 copy-start.2
  24.1 18.4 %all_to_all.15.gathered = f32[32,16,128]{2,1,0:T(8,128)S(1)} all-to-all(f32[32,16,128]{2,1,0:T(8,128)S(1)} %get-tuple-element.19), channel_id=1, replica_groups=mesh['asset'=32,'tm'=4] {'asset'}, dimensions={0} | all-to-all | bytes 524288 | tf_op jit(solution)/shard_map/all_to_all | solution.py:464
  42.5 5.3 %second_pass.1 = (f32[3,8,128]{2,1,0:T(8,128)S(1)}, f32[16,128]{1,0:T(8,128)S(1)}) custom-call(f32[32,16,128]{2,1,0:T(8,128)S(1)} %all_to_all.15.gathered, f32[4,288,2048]{2,1,0:T(8,128)S(1)} %get-tuple-element.17.buf, f32[288,2048]{1,0:T(8,128)S(1)} %get-tuple-element.18.inverse), custom_call_target="tpu_custom_call" | custom-call | flops 20971520 | tf_op jit(solution)/shard_map/second_pass/pallas_call | solution.py:465
  47.8 0.0 collective-permute-done.2.head
  47.8 0.0 collective-permute-done.1.tail
  47.8 0.0 copy-done.2
  47.8 2.9 %late_first_pass.1 = (f32[4,64,2048]{2,1,0:T(8,128)S(1)}, f32[4,8,2048]{2,1,0:T(8,128)S(1)}, f32[32,16,128]{2,1,0:T(8,128)S(1)}) custom-call(s32[2]{0:T(128)S(1)} %pad_add_fusion.times, f32[4,288,2048]{2,1,0:T(8,128)S(1)} %get-tuple-element.17.buf, f32[4,32,2048]{2,1,0:T(8,128)S(1)} %collective-permute-done.1.tail, ...), custom_call_target="tpu_custom_call" | custom-call | flops 10485760 | tf_op jit(solution)/shard_map/late_first_pass/pallas_call | solution.py:469
  50.8 12.4 %all_to_all.16.gathered = f32[32,16,128]{2,1,0:T(8,128)S(1)} all-to-all(f32[32,16,128]{2,1,0:T(8,128)S(1)} %get-tuple-element.22), channel_id=1, replica_groups=mesh['asset'=32,'tm'=4] {'asset'}, dimensions={0} | all-to-all | bytes 524288 | tf_op jit(solution)/shard_map/all_to_all | solution.py:474
  63.2 1.8 %late_second_pass.1 = (f32[2,8,128]{2,1,0:T(8,128)S(1)}, f32[32,8,128]{2,1,0:T(8,128)S(1)}) custom-call(f32[32,16,128]{2,1,0:T(8,128)S(1)} %all_to_all.16.gathered, f32[3,8,128]{2,1,0:T(8,128)S(1)} %get-tuple-element.23.stats, f32[4,64,2048]{2,1,0:T(8,128)S(1)} %get-tuple-element.24.late, f32[288,2048]{1,0:T(8,128)S(1)} %get-tuple-element.18.inverse), custom_call_target="tpu_custom_call" | custom-call | flops 6291456 | tf_op jit(solution)/shard_map/late_second_pass/pallas_call | solution.py:475
  65.0 11.1 %all_to_all.17.gathered = f32[32,8,128]{2,1,0:T(8,128)S(1)} all-to-all(f32[32,8,128]{2,1,0:T(8,128)S(1)} %get-tuple-element.25), channel_id=1, replica_groups=mesh['asset'=32,'tm'=4] {'asset'}, dimensions={0} | all-to-all | bytes 262144 | tf_op jit(solution)/shard_map/all_to_all | solution.py:479
  76.1 0.1 send_pass.1
  76.3 1.2 %collective-permute-start.3 = (f32[8,128]{1,0:T(8,128)S(1)}, f32[8,128]{1,0:T(8,128)S(1)}, u32[]{:S(2)}, u32[]{:S(2)}) collective-permute-start(f32[8,128]{1,0:T(8,128)S(1)} %get-tuple-element.27), channel_id=1, source_target_pairs={{0,1},{1,2},{2,3},{3,0},{4,5},{5,6},{6,7},{7,4},{8,9},{9,10},{10,1... | collective-permute-start | bytes 12296 | tf_op jit(solution)/shard_map/ppermute | solution.py:492
  77.5 10.1 %main_final_pass.1.prior = f32[4,256,2048]{2,1,0:T(8,128)} custom-call(f32[4,288,2048]{2,1,0:T(8,128)S(1)} %get-tuple-element.17.buf, f32[288,2048]{1,0:T(8,128)S(1)} %get-tuple-element.18.inverse, f32[3,8,128]{2,1,0:T(8,128)S(1)} %get-tuple-element.23.stats, f32[2,8,128]{2,1,0:T(8,128)S(1)} %get-tuple-element.26.level), custom_call_target="tpu_custom_call" | custom-call | flops 20971520 | tf_op jit(solution)/shard_map/main_final_pass/pallas_call | solution.py:480
  87.6 2.2 %late_final_pass.1.prior = f32[4,256,2048]{2,1,0:T(8,128)} custom-call(f32[4,64,2048]{2,1,0:T(8,128)S(1)} %get-tuple-element.24.late, f32[288,2048]{1,0:T(8,128)S(1)} %get-tuple-element.18.inverse, f32[2,8,128]{2,1,0:T(8,128)S(1)} %get-tuple-element.26.level, f32[2,8,128]{2,1,0:T(8,128)S(1)} %get-tuple-element.28.level4, ...), custom_call_target="tpu_custom_call", output_to_operand_aliasing={{}: (4, {})} | custom-call | flops 4194304 | tf_op jit(solution)/shard_map/late_final_pass/pallas_call | solution.py:497
  89.8 0.0 collective-permute-done.tail
  89.8 0.0 collective-permute-done.3.sent
  89.8 2.8 %head_final_pass.1 = f32[4,256,2048]{2,1,0:T(8,128)} custom-call(s32[2]{0:T(128)S(1)} %pad_add_fusion.times, f32[4,288,2048]{2,1,0:T(8,128)S(1)} %get-tuple-element.17.buf, f32[4,32,2048]{2,1,0:T(8,128)S(1)} %collective-permute-done.tail, f32[4,8,2048]{2,1,0:T(8,128)S(1)} %get-tuple-element.21.whole, ...), custom_call_target="tpu_custom_call", output_to_operand_aliasing={{}: (7, {})} | custom-call | flops 4194304 | tf_op jit(solution)/shard_map/head_final_pass/pallas_call | solution.py:501
Async XLA Ops:
  3.7 44.1 %collective-permute-start.2 = (f32[4,32,2048]{2,1,0:T(8,128)}, f32[4,32,2048]{2,1,0:T(8,128)S(1)}, u32[]{:S(2)}, u32[]{:S(2)}) collective-permute-start(f32[4,32,2048]{2,1,0:T(8,128)} %get-tuple-element.29), channel_id=1, source_target_pairs={{1,0},{2,1},{3,2},{0,3},{5,4},{6,5},{7,6},{4,7},{9,8},{10,9},{11,1... | collective-permute-start | bytes 3145736 | tf_op jit(solution)/shard_map/ppermute | solution.py:438
  6.9 40.8 %collective-permute-start.1 = (f32[4,32,2048]{2,1,0:T(8,128)}, f32[4,32,2048]{2,1,0:T(8,128)S(1)}, u32[]{:S(2)}, u32[]{:S(2)}) collective-permute-start(f32[4,32,2048]{2,1,0:T(8,128)} %get-tuple-element.31), channel_id=1, source_target_pairs={{0,1},{1,2},{2,3},{4,5},{5,6},{6,7},{8,9},{9,10},{10,11},{12,13},{... | collective-permute-start | bytes 3145736 | tf_op jit(solution)/shard_map/ppermute | solution.py:437
  8.3 81.5 %collective-permute-start = (f32[4,32,2048]{2,1,0:T(8,128)}, f32[4,32,2048]{2,1,0:T(8,128)S(1)}, u32[]{:S(2)}, u32[]{:S(2)}) collective-permute-start(f32[4,32,2048]{2,1,0:T(8,128)} %get-tuple-element.30), channel_id=1, source_target_pairs={{0,1},{1,2},{2,3},{4,5},{5,6},{6,7},{8,9},{9,10},{10,11},{12,13},{... | collective-permute-start | bytes 3145736 | tf_op jit(solution)/shard_map/ppermute | solution.py:439
  11.1 3.4 %copy-start = (f32[4,256,2048]{2,1,0:T(8,128)S(1)}, f32[4,256,2048]{2,1,0:T(8,128)}, u32[]{:S(2)}) copy-start(f32[4,256,2048]{2,1,0:T(8,128)} %x_hbm.1) | copy-start | bytes 25165828
  14.5 0.7 copy-start.1
  15.2 0.7 copy-start.3
  24.1 23.7 %copy-start.2 = (s32[2048]{0:T(1024)S(1)}, s32[2048]{0:T(1024)}, u32[]{:S(2)}) copy-start(s32[2048]{0:T(1024)} %param.4) | copy-start | bytes 24580
  76.3 13.5 %collective-permute-start.3 = (f32[8,128]{1,0:T(8,128)S(1)}, f32[8,128]{1,0:T(8,128)S(1)}, u32[]{:S(2)}, u32[]{:S(2)}) collective-permute-start(f32[8,128]{1,0:T(8,128)S(1)} %get-tuple-element.27), channel_id=1, source_target_pairs={{0,1},{1,2},{2,3},{3,0},{4,5},{5,6},{6,7},{7,4},{8,9},{9,10},{10,1... | collective-permute-start | bytes 12296 | tf_op jit(solution)/shard_map/ppermute | solution.py:492

commit v2 on v1

--- a/solution.py
+++ b/solution.py
@@ -16,13 +16,17 @@
 LATE_GROUPS = LATE // GROUP
 SKIP_GROUPS = WINDOW // GROUP
 VMEM = pl.BlockSpec(memory_space=pltpu.VMEM)
-SMEM = pl.BlockSpec(memory_space=pltpu.SMEM)
-ANY = pl.BlockSpec(memory_space=pl.ANY)
+HBM = pl.BlockSpec(memory_space=pltpu.HBM)
 MIB = 1 << 20
 
 
 def rows_of(g):
     return pl.ds(g * GROUP, GROUP)
+
+
+def block_starts(rows):
+    block, blocks = lax.axis_index("tm"), lax.axis_size("tm")
+    return block * rows, lax.rem(block + 1, blocks) * rows
 
 
 def sublanes(width):
@@ -78,23 +82,40 @@
     return out, carried
 
 
-def first_pass(times, x_hbm, from_ref, until_ref, buf, inverse, pay, xs, sums, counts, sems):
-    fields, rows, assets = x_hbm.shape
+def load(x_hbm, near, head, x_ref, sems):
+    rows = x_hbm.shape[1]
+    copies = [
+        pltpu.make_async_copy(x_hbm.at[:, pl.ds(rows - LATE, LATE), :], near, sems.at[0]),
+        pltpu.make_async_copy(x_hbm.at[:, pl.ds(0, LATE), :], head, sems.at[1]),
+        pltpu.make_async_copy(x_hbm, x_ref, sems.at[2]),
+    ]
+    for copy in copies:
+        copy.start()
+    for copy in copies:
+        copy.wait()
+
+
+def first_pass(
+    x_ref, from_hbm, until_hbm,
+    buf, inverse, pay, far, from_ref, until_ref, sums, counts, date_sems,
+):
+    fields, rows, assets = x_ref.shape
     own_groups = rows // GROUP
     groups = own_groups + LATE_GROUPS
     main = own_groups - SKIP_GROUPS
-    chunks, _, _, width = xs.shape
-    base, base_next = times[0], times[1]
-
-    def fetch(c):
-        lanes = pl.ds(pl.multiple_of(c * width, width), width)
-        return pltpu.make_async_copy(x_hbm.at[:, :, lanes], xs.at[c], sems.at[c])
-
-    for c in range(chunks):
-        fetch(c).start()
+    width = 2 * LANE
+    base, base_next = block_starts(rows)
+    dates = [
+        pltpu.make_async_copy(from_hbm, from_ref, date_sems.at[0]),
+        pltpu.make_async_copy(until_hbm, until_ref, date_sems.at[1]),
+    ]
+    for copy in dates:
+        copy.start()
     sums[...] = jnp.zeros_like(sums)
     counts[...] = jnp.zeros_like(counts)
     sub = sublanes(width)
+    for copy in dates:
+        copy.wait()
 
     def chunk(c, carry):
         lanes = pl.ds(pl.multiple_of(c * width, width), width)
@@ -111,15 +132,17 @@
             if g >= SKIP_GROUPS - LATE_GROUPS:
                 which = g - (SKIP_GROUPS - LATE_GROUPS)
                 counts[which] += folded(jnp.where(listed, 1.0, 0.0))
-        fetch(c).wait()
         start = base + age
 
         def one_field(f, carry):
             last1 = last2 = last4 = last8 = None
             last16, last32 = [], []
             for g in range(groups):
+                if own_groups - SKIP_GROUPS <= g < own_groups - LATE_GROUPS:
+                    to = rows_of(g - (own_groups - SKIP_GROUPS))
+                    far[f, to, lanes] = x_ref[f, rows_of(g), lanes]
                 if g < own_groups:
-                    x = jnp.where(start >= -g * GROUP, xs[c, f, rows_of(g), :], 0.0)
+                    x = jnp.where(start >= -g * GROUP, x_ref[f, rows_of(g), lanes], 0.0)
                 else:
                     x = jnp.zeros((GROUP, width), jnp.float32)
                 r = pltpu.roll(x, 1, 0)
@@ -147,7 +170,7 @@
         lax.fori_loop(0, fields, one_field, 0)
         return carry
 
-    lax.fori_loop(0, chunks, chunk, 0)
+    lax.fori_loop(0, assets // width, chunk, 0)
     lane = lanes_iota()
     tiles = [jnp.zeros((GROUP, LANE), jnp.float32) for _ in range(2)]
     for stat in range(2):
@@ -168,6 +191,25 @@
         pay[d, GROUP:, :] = tiles[1]
 
 
+def row_moments(source, mine, inverse, where, cs, ss):
+    fields, _, assets = source.shape
+    width = 2 * LANE
+    acc = [None] * (2 * fields)
+
+    def added(i, x):
+        acc[i] = x if acc[i] is None else acc[i] + x
+
+    for at in range(0, assets, width):
+        lanes = pl.ds(at, width)
+        listed = inverse[where, lanes] > 0.0
+        for f in range(fields):
+            z = clipped_score(source[f, mine, lanes], cs[f], ss[f])
+            z = jnp.where(listed, z, 0.0)
+            added(f, folded(z))
+            added(fields + f, folded(z * z))
+    return acc
+
+
 def second_pass(gathered, buf, inverse, stats, part):
     fields, _, assets = buf.shape
     main = (inverse.shape[0] - LATE) // GROUP - SKIP_GROUPS
@@ -182,26 +224,14 @@
     present = jnp.maximum(present, 1.0)
     center, scale = moments(t0, t1, present)
     stats[0], stats[1], stats[2] = center, scale, present
-    width = 4 * LANE
+    width = 2 * LANE
     tiles = [jnp.zeros((GROUP, LANE), jnp.float32) for _ in range(2)]
     for g in range(main):
         rows = rows_of(g + SKIP_GROUPS)
         cs = [column(center, f * main + g, width) for f in range(fields)]
         ss = [column(scale, f * main + g, width) for f in range(fields)]
 
-        def tile(i, acc):
-            lanes = pl.ds(pl.multiple_of(i * width, width), width)
-            listed = inverse[rows, lanes] > 0.0
-            acc = list(acc)
-            for f in range(fields):
-                z = clipped_score(buf[f, rows, lanes], cs[f], ss[f])
-                z = jnp.where(listed, z, 0.0)
-                acc[f] = acc[f] + folded(z)
-                acc[fields + f] = acc[fields + f] + folded(z * z)
-            return tuple(acc)
-
-        zero = jnp.zeros((GROUP, LANE), jnp.float32)
-        acc = lax.fori_loop(0, assets // width, tile, (zero,) * (2 * fields))
+        acc = row_moments(buf, rows, inverse, rows, cs, ss)
         for f in range(fields):
             for stat in range(2):
                 tiles[stat] = jnp.where(
@@ -211,12 +241,12 @@
     part[GROUP:, :] = tiles[1]
 
 
-def late_first_pass(times, buf, tail, head, from_ref, inverse, part, late, whole, pay):
+def late_first_pass(buf, tail, head, from_ref, inverse, part, late, whole, pay):
     fields, _, assets = buf.shape
     rows = inverse.shape[0] - LATE
-    base, base_next = times[0], times[1]
+    base, base_next = block_starts(rows)
     follows = jnp.where(base_next > 0, 1.0, 0.0)
-    width = LANE
+    width = 4 * LANE
     sub = sublanes(width)
     lane = lanes_iota()
     first = LANE - 2 * fields * LATE_GROUPS
@@ -246,8 +276,8 @@
                     r = r * inverse[where, lanes]
                     late[f, rows_of(side * LATE_GROUPS + g), lanes] = r
                     k = side * LATE_GROUPS + g
-                    acc[k] = acc[k] + r
-                    acc[2 * LATE_GROUPS + k] = acc[2 * LATE_GROUPS + k] + r * r
+                    acc[k] = acc[k] + folded(r)
+                    acc[2 * LATE_GROUPS + k] = acc[2 * LATE_GROUPS + k] + folded(r * r)
             return tuple(acc)
 
         zero = jnp.zeros((GROUP, LANE), jnp.float32)
@@ -269,7 +299,7 @@
     total = summed(gathered)
     center, scale = moments(total[:GROUP], total[GROUP:], stats[2])
     level[0], level[1] = center, scale
-    width = 4 * LANE
+    width = 2 * LANE
     first = LANE - 2 * fields * LATE_GROUPS
     lane = lanes_iota()
     out = jnp.zeros((GROUP, LANE), jnp.float32)
@@ -281,19 +311,7 @@
             where = rows_of(LATE_GROUPS + g if side == 0 else rows // GROUP + g)
             mine = rows_of(side * LATE_GROUPS + g)
 
-            def tile(i, acc):
-                lanes = pl.ds(pl.multiple_of(i * width, width), width)
-                listed = inverse[where, lanes] > 0.0
-                acc = list(acc)
-                for f in range(fields):
-                    z = clipped_score(late[f, mine, lanes], cs[f], ss[f])
-                    z = jnp.where(listed, z, 0.0)
-                    acc[f] = acc[f] + folded(z)
-                    acc[fields + f] = acc[fields + f] + folded(z * z)
-                return tuple(acc)
-
-            zero = jnp.zeros((GROUP, LANE), jnp.float32)
-            acc = lax.fori_loop(0, assets // width, tile, (zero,) * (2 * fields))
+            acc = row_moments(late, mine, inverse, where, cs, ss)
             back = LANE - first
             for f in range(fields):
                 out = jnp.where(lane == spots[f], total_of(acc[f]), out)
@@ -303,23 +321,19 @@
 
 
 def final_rows(f, where, source, mine, inverse, stage, put, cols, assets):
-    width = 4 * LANE
+    width = 2 * LANE
     c1, s1, c2, s2 = cols
-
-    def tile(i, carry):
-        lanes = pl.ds(pl.multiple_of(i * width, width), width)
+    for at in range(0, assets, width):
+        lanes = pl.ds(at, width)
         z = clipped_score(source[f, mine, lanes], c1, s1)
         z = (z - c2) * s2
         stage[f, put, lanes] = jnp.where(inverse[where, lanes] > 0.0, z, 0.0)
-        return carry
-
-    lax.fori_loop(0, assets // width, tile, 0)
 
 
 def main_final_pass(buf, inverse, stats, level, out, stage, sems):
     fields, rows, assets = out.shape
     main = rows // GROUP - SKIP_GROUPS
-    width = 4 * LANE
+    width = 2 * LANE
     c1, s1, c2, s2 = stats[0], stats[1], level[0], level[1]
     copies = []
     for f in range(fields):
@@ -353,7 +367,7 @@
 
 def late_final_pass(late, inverse, level, level4, prior, out, stage, sems):
     fields, _, assets = late.shape
-    width = 4 * LANE
+    width = 2 * LANE
     first = LANE - 2 * fields * LATE_GROUPS
     copies = []
     for f in range(fields):
@@ -370,10 +384,10 @@
         copy.wait()
 
 
-def head_final_pass(times, buf, tail, whole, from_ref, inverse, sent, prior, out, stage, sems):
+def head_final_pass(buf, tail, whole, from_ref, inverse, sent, prior, out, stage, sems):
     fields, _, assets = buf.shape
-    base = times[0]
-    width = 2 * LANE
+    base = block_starts(inverse.shape[0] - LATE)[0]
+    width = 4 * LANE
     sub = sublanes(width)
     levels = sent[...]
     copies = []
@@ -430,47 +444,52 @@
     fields, rows, assets = values.shape
     n = lax.axis_size("asset")
     blocks = lax.axis_size("tm")
-    block = lax.axis_index("tm")
     forward = [(i, i + 1) for i in range(blocks - 1)]
     ring = [(i, (i + 1) % blocks) for i in range(blocks)]
     back = [((i + 1) % blocks, i) for i in range(blocks)]
-    tail_near = lax.ppermute(values[:, rows - LATE :], "tm", forward)
-    head = lax.ppermute(values[:, :LATE], "tm", back)
-    tail_far = lax.ppermute(values[:, rows - WINDOW : rows - LATE], "tm", forward)
-    times = jnp.stack([block * rows, lax.rem(block + 1, blocks) * rows]).astype(jnp.int32)
+    work = fields * rows * assets
+    slab = shape(fields, LATE, assets)
+    near, head, held = call(
+        load, "load", [HBM], (slab, slab, shape(fields, rows, assets)), (VMEM,) * 3,
+        [pltpu.SemaphoreType.DMA((3,))], limit=40, flops=work // 8,
+    )(values)
+    tail_near = lax.ppermute(near, "tm", forward)
+    head = lax.ppermute(head, "tm", back)
     opened, closed = listed_from.reshape(1, assets), listed_until.reshape(1, assets)
     main = rows // GROUP - SKIP_GROUPS
-    width = 2 * LANE
-    chunks = assets // width
     tile = shape(GROUP, LANE)
     pair = shape(2, GROUP, LANE)
     exchange = functools.partial(
         lax.all_to_all, axis_name="asset", split_axis=0, concat_axis=0, tiled=True
     )
-    work = fields * rows * assets
-
-    buf, inverse, pay = call(
-        first_pass, "first_pass", [SMEM, ANY, VMEM, VMEM],
-        (shape(fields, rows + LATE, assets), shape(rows + LATE, assets), shape(n, 2 * GROUP, LANE)),
-        (VMEM, VMEM, VMEM),
+
+    buf, inverse, pay, far = call(
+        first_pass, "first_pass", [VMEM, HBM, HBM],
+        (
+            shape(fields, rows + LATE, assets), shape(rows + LATE, assets),
+            shape(n, 2 * GROUP, LANE), slab,
+        ),
+        (VMEM,) * 4,
         [
-            pltpu.VMEM((chunks, fields, rows, width), jnp.float32),
+            pltpu.VMEM((1, assets), jnp.int32),
+            pltpu.VMEM((1, assets), jnp.int32),
             pltpu.VMEM((2, fields, main, GROUP, LANE), jnp.float32),
             pltpu.VMEM((main + 2 * LATE_GROUPS, GROUP, LANE), jnp.float32),
-            pltpu.SemaphoreType.DMA((chunks,)),
+            pltpu.SemaphoreType.DMA((2,)),
         ],
-        limit=26, flops=20 * work,
-    )(times, values, opened, closed)
+        limit=8, flops=20 * work,
+    )(held, opened, closed)
+    tail_far = lax.ppermute(far, "tm", forward)
     gathered = exchange(pay)
     stats, part = call(
         second_pass, "second_pass", [VMEM] * 3,
         (shape(3, GROUP, LANE), shape(2 * GROUP, LANE)), (VMEM, VMEM), limit=16, flops=10 * work,
     )(gathered, buf, inverse)
     late, whole, pay = call(
-        late_first_pass, "late_first_pass", [SMEM] + [VMEM] * 6,
+        late_first_pass, "late_first_pass", [VMEM] * 6,
         (shape(fields, 2 * LATE, assets), shape(fields, GROUP, assets), shape(n, 2 * GROUP, LANE)),
         (VMEM, VMEM, VMEM), limit=20, flops=5 * work,
-    )(times, buf, tail_near, head, opened, inverse, part)
+    )(buf, tail_near, head, opened, inverse, part)
     gathered = exchange(pay)
     level, pay = call(
         late_second_pass, "late_second_pass", [VMEM] * 4,
@@ -479,7 +498,7 @@
     gathered = exchange(pay)
     out = call(
         main_final_pass, "main_final_pass", [VMEM] * 4,
-        shape(fields, rows, assets), ANY,
+        shape(fields, rows, assets), HBM,
         [
             pltpu.VMEM((fields, rows - WINDOW, assets), jnp.float32),
             pltpu.SemaphoreType.DMA((fields,)),
@@ -495,13 +514,13 @@
         pltpu.SemaphoreType.DMA((fields,)),
     ]
     out = call(
-        late_final_pass, "late_final_pass", [VMEM] * 4 + [ANY],
-        shape(fields, rows, assets), ANY, stage, limit=16, flops=2 * work, aliases={4: 0},
+        late_final_pass, "late_final_pass", [VMEM] * 4 + [HBM],
+        shape(fields, rows, assets), HBM, stage, limit=16, flops=2 * work, aliases={4: 0},
     )(late, inverse, level, level4, out)
     return call(
-        head_final_pass, "head_final_pass", [SMEM] + [VMEM] * 6 + [ANY],
-        shape(fields, rows, assets), ANY, stage, limit=16, flops=2 * work, aliases={7: 0},
-    )(times, buf, tail_far, whole, opened, inverse, sent, out)
+        head_final_pass, "head_final_pass", [VMEM] * 6 + [HBM],
+        shape(fields, rows, assets), HBM, stage, limit=16, flops=2 * work, aliases={6: 0},
+    )(buf, tail_far, whole, opened, inverse, sent, out)
 
 
 def solution(mesh):

time: 93 us -> 74 us (0.80)
  Pallas kernels: 33.5 us -> 23.1 us
  local copies, waits for them, and re-layouts: 8.43 us -> 0.01 us
    pallas_call x1, Pallas kernels: 10.1 us -> 3.16 us  [per_device(): call(main_final_pass, 'main_final_pass', [VMEM] * 4, shape(fields, rows,...]
    unnamed x8 -> x4, local copies, waits for them, and re-layouts: 4.78 us -> 0.01 us
    slice x1 -> x0, local copies, waits for them, and re-layouts: 3.65 us -> none  [per_device(): head = lax.ppermute(values[:, :LATE], 'tm', back)]
    pallas_call x1, Pallas kernels: 5.29 us -> 3.25 us  [per_device(): call(second_pass, 'second_pass', [VMEM] * 3, (shape(3, GROUP, LANE), shap...]
    pallas_call x4 -> x5, Pallas kernels: 16.2 us -> 15.6 us  [the longest x1 6.5 us: per_device(): call(first_pass, 'first_pass', [VMEM, HBM, HBM], (shape(fields, rows + LA...]
  transfers between devices with their start and end apart: 4 -> 4, of which waited for: 0 -> 0; matrix products, arithmetic and copies ran while one was open for 0% -> 0% of each run, Pallas kernels for 33% -> 23%
where the time goes in v2:
time: 74 us; the launch traced here: 73.8 us
  blocking collectives  42 us (57%)
  Pallas kernels  23.1 us (31%)
  starting transfers between devices  8.63 us (12%)
    all_to_all x3, blocking collectives, per_device(): gathered = exchange(pay)  42 us
    pallas_call x1, Pallas kernels, per_device(): call(first_pass, 'first_pass', [VMEM, HBM, HBM], (shape(fields, rows + LA...  6.5 us
    pallas_call x1, Pallas kernels, per_device(): call(load, 'load', [HBM], (slab, slab, shape(fields, rows, assets)), (VME...  4.08 us
    ppermute x1, starting transfers between devices, per_device(): tail_near = lax.ppermute(near, 'tm', forward)  4 us
    pallas_call x1, Pallas kernels, per_device(): call(second_pass, 'second_pass', [VMEM] * 3, (shape(3, GROUP, LANE), shap...  3.25 us
    pallas_call x1, Pallas kernels, per_device(): call(main_final_pass, 'main_final_pass', [VMEM] * 4, shape(fields, rows,...  3.16 us
    ppermute x1, starting transfers between devices, per_device(): tail_far = lax.ppermute(far, 'tm', forward)  2.85 us
    pallas_call x1, Pallas kernels, per_device(): call(head_final_pass, 'head_final_pass', [VMEM] * 6 + [HBM], shape(fields...  2.03 us
  transfers between devices with their start and end apart: 4, of which 0 were waited for; matrix products, arithmetic and copies ran while one was open for 0% of the time, Pallas kernels for 23%

profile of v2, /device:TPU:1, one launch (start us, length us, event | category | flops | bytes accessed | tf_op | source)
XLA Modules:
  0.0 73.8 jit_solution(2164019152127487494)
XLA Ops:
  0.0 0.0 copy-start.1
  0.0 0.0 copy-start
  0.0 4.1 %load.1 = (f32[4,32,2048]{2,1,0:T(8,128)S(1)}, f32[4,32,2048]{2,1,0:T(8,128)S(1)}, f32[4,256,2048]{2,1,0:T(8,128)S(1)}) custom-call(f32[4,256,2048]{2,1,0:T(8,128)} %x_hbm.1), custom_call_target="tpu_custom_call" | custom-call | flops 262144 | tf_op jit(solution)/shard_map/load/pallas_call | solution.py:452
  4.1 4.0 %collective-permute-start.1 = (f32[4,32,2048]{2,1,0:T(8,128)S(1)}, f32[4,32,2048]{2,1,0:T(8,128)S(1)}, u32[]{:S(2)}, u32[]{:S(2)}) collective-permute-start(f32[4,32,2048]{2,1,0:T(8,128)S(1)} %get-tuple-element.24), channel_id=1, source_target_pairs={{0,1},{1,2},{2,3},{4,5},{5,6},{6,7},{8,9},{9,10},{10,11},{12,13},{... | collective-permute-start | bytes 3145736 | tf_op jit(solution)/shard_map/ppermute | solution.py:456
  8.1 0.7 collective-permute-start.2
  8.8 0.0 copy-done.1
  8.8 0.0 copy-done
  8.8 6.5 %first_pass.1 = (f32[4,288,2048]{2,1,0:T(8,128)S(1)}, f32[288,2048]{1,0:T(8,128)S(1)}, f32[32,16,128]{2,1,0:T(8,128)S(1)}, f32[4,32,2048]{2,1,0:T(8,128)S(1)}) custom-call(f32[4,256,2048]{2,1,0:T(8,128)S(1)} %get-tuple-element.21.x_ref, s32[1,2048]{1,0:T(1,128)S(1)} %bitcast.2, s32[1,2048]{1,0:T(1,128)S(1)} %bitcast.5), custom_call_target="tpu_custom_call" | custom-call | flops 41943040 | tf_op jit(solution)/shard_map/first_pass/pallas_call | solution.py:466
  15.3 2.8 %collective-permute-start = (f32[4,32,2048]{2,1,0:T(8,128)S(1)}, f32[4,32,2048]{2,1,0:T(8,128)S(1)}, u32[]{:S(2)}, u32[]{:S(2)}) collective-permute-start(f32[4,32,2048]{2,1,0:T(8,128)S(1)} %get-tuple-element.23), channel_id=1, source_target_pairs={{0,1},{1,2},{2,3},{4,5},{5,6},{6,7},{8,9},{9,10},{10,11},{12,13},{... | collective-permute-start | bytes 3145736 | tf_op jit(solution)/shard_map/ppermute | solution.py:482
  18.1 18.4 %all_to_all.15.gathered = f32[32,16,128]{2,1,0:T(8,128)S(1)} all-to-all(f32[32,16,128]{2,1,0:T(8,128)S(1)} %get-tuple-element.27), channel_id=1, replica_groups=mesh['asset'=32,'tm'=4] {'asset'}, dimensions={0} | all-to-all | bytes 524288 | tf_op jit(solution)/shard_map/all_to_all | solution.py:483
  36.5 3.2 %second_pass.1 = (f32[3,8,128]{2,1,0:T(8,128)S(1)}, f32[16,128]{1,0:T(8,128)S(1)}) custom-call(f32[32,16,128]{2,1,0:T(8,128)S(1)} %all_to_all.15.gathered, f32[4,288,2048]{2,1,0:T(8,128)S(1)} %get-tuple-element.22.buf, f32[288,2048]{1,0:T(8,128)S(1)} %get-tuple-element.26.inverse), custom_call_target="tpu_custom_call" | custom-call | flops 20971520 | tf_op jit(solution)/shard_map/second_pass/pallas_call | solution.py:484
  39.7 0.0 collective-permute-done.1.tail
  39.8 0.0 collective-permute-done.2.head
  39.8 1.9 %late_first_pass.1 = (f32[4,64,2048]{2,1,0:T(8,128)S(1)}, f32[4,8,2048]{2,1,0:T(8,128)S(1)}, f32[32,16,128]{2,1,0:T(8,128)S(1)}) custom-call(f32[4,288,2048]{2,1,0:T(8,128)S(1)} %get-tuple-element.22.buf, f32[4,32,2048]{2,1,0:T(8,128)S(1)} %collective-permute-done.1.tail, f32[4,32,2048]{2,1,0:T(8,128)S(1)} %collective-permute-done.2.head, ...), custom_call_target="tpu_custom_call" | custom-call | flops 10485760 | tf_op jit(solution)/shard_map/late_first_pass/pallas_call | solution.py:488
  41.6 12.4 %all_to_all.16.gathered = f32[32,16,128]{2,1,0:T(8,128)S(1)} all-to-all(f32[32,16,128]{2,1,0:T(8,128)S(1)} %get-tuple-element.30), channel_id=1, replica_groups=mesh['asset'=32,'tm'=4] {'asset'}, dimensions={0} | all-to-all | bytes 524288 | tf_op jit(solution)/shard_map/all_to_all | solution.py:493
  54.0 1.0 %late_second_pass.1 = (f32[2,8,128]{2,1,0:T(8,128)S(1)}, f32[32,8,128]{2,1,0:T(8,128)S(1)}) custom-call(f32[32,16,128]{2,1,0:T(8,128)S(1)} %all_to_all.16.gathered, f32[3,8,128]{2,1,0:T(8,128)S(1)} %get-tuple-element.31.stats, f32[4,64,2048]{2,1,0:T(8,128)S(1)} %get-tuple-element.32.late, f32[288,2048]{1,0:T(8,128)S(1)} %get-tuple-element.26.inverse), custom_call_target="tpu_custom_call" | custom-call | flops 6291456 | tf_op jit(solution)/shard_map/late_second_pass/pallas_call | solution.py:494
  55.0 11.1 %all_to_all.17.gathered = f32[32,8,128]{2,1,0:T(8,128)S(1)} all-to-all(f32[32,8,128]{2,1,0:T(8,128)S(1)} %get-tuple-element.33), channel_id=1, replica_groups=mesh['asset'=32,'tm'=4] {'asset'}, dimensions={0} | all-to-all | bytes 262144 | tf_op jit(solution)/shard_map/all_to_all | solution.py:498
  66.2 0.1 send_pass.1
  66.3 1.1 %collective-permute-start.3 = (f32[8,128]{1,0:T(8,128)S(1)}, f32[8,128]{1,0:T(8,128)S(1)}, u32[]{:S(2)}, u32[]{:S(2)}) collective-permute-start(f32[8,128]{1,0:T(8,128)S(1)} %get-tuple-element.35), channel_id=1, source_target_pairs={{0,1},{1,2},{2,3},{3,0},{4,5},{5,6},{6,7},{7,4},{8,9},{9,10},{10,1... | collective-permute-start | bytes 12296 | tf_op jit(solution)/shard_map/ppermute | solution.py:511
  67.4 3.2 %main_final_pass.1.prior = f32[4,256,2048]{2,1,0:T(8,128)} custom-call(f32[4,288,2048]{2,1,0:T(8,128)S(1)} %get-tuple-element.22.buf, f32[288,2048]{1,0:T(8,128)S(1)} %get-tuple-element.26.inverse, f32[3,8,128]{2,1,0:T(8,128)S(1)} %get-tuple-element.31.stats, f32[2,8,128]{2,1,0:T(8,128)S(1)} %get-tuple-element.34.level), custom_call_target="tpu_custom_call" | custom-call | flops 20971520 | tf_op jit(solution)/shard_map/main_final_pass/pallas_call | solution.py:499
  70.6 1.1 %late_final_pass.1.prior = f32[4,256,2048]{2,1,0:T(8,128)} custom-call(f32[4,64,2048]{2,1,0:T(8,128)S(1)} %get-tuple-element.32.late, f32[288,2048]{1,0:T(8,128)S(1)} %get-tuple-element.26.inverse, f32[2,8,128]{2,1,0:T(8,128)S(1)} %get-tuple-element.34.level, f32[2,8,128]{2,1,0:T(8,128)S(1)} %get-tuple-element.36.level4, ...), custom_call_target="tpu_custom_call", output_to_operand_aliasing={{}: (4, {})} | custom-call | flops 4194304 | tf_op jit(solution)/shard_map/late_final_pass/pallas_call | solution.py:516
  71.7 0.0 collective-permute-done.tail
  71.8 0.0 collective-permute-done.3.sent
  71.8 2.0 %head_final_pass.1 = f32[4,256,2048]{2,1,0:T(8,128)} custom-call(f32[4,288,2048]{2,1,0:T(8,128)S(1)} %get-tuple-element.22.buf, f32[4,32,2048]{2,1,0:T(8,128)S(1)} %collective-permute-done.tail, f32[4,8,2048]{2,1,0:T(8,128)S(1)} %get-tuple-element.29.whole, s32[1,2048]{1,0:T(1,128)S(1)} %bitcast.4, ...), custom_call_target="tpu_custom_call", output_to_operand_aliasing={{}: (6, {})} | custom-call | flops 4194304 | tf_op jit(solution)/shard_map/head_final_pass/pallas_call | solution.py:520
Async XLA Ops:
  0.0 8.8 %copy-start.1 = (s32[2048]{0:T(1024)S(1)}, s32[2048]{0:T(1024)}, u32[]{:S(2)}) copy-start(s32[2048]{0:T(1024)} %param.5) | copy-start | bytes 24580
  0.0 8.8 %copy-start = (s32[2048]{0:T(1024)S(1)}, s32[2048]{0:T(1024)}, u32[]{:S(2)}) copy-start(s32[2048]{0:T(1024)} %param.4) | copy-start | bytes 24580
  4.1 35.7 %collective-permute-start.1 = (f32[4,32,2048]{2,1,0:T(8,128)S(1)}, f32[4,32,2048]{2,1,0:T(8,128)S(1)}, u32[]{:S(2)}, u32[]{:S(2)}) collective-permute-start(f32[4,32,2048]{2,1,0:T(8,128)S(1)} %get-tuple-element.24), channel_id=1, source_target_pairs={{0,1},{1,2},{2,3},{4,5},{5,6},{6,7},{8,9},{9,10},{10,11},{12,13},{... | collective-permute-start | bytes 3145736 | tf_op jit(solution)/shard_map/ppermute | solution.py:456
  8.1 31.7 %collective-permute-start.2 = (f32[4,32,2048]{2,1,0:T(8,128)S(1)}, f32[4,32,2048]{2,1,0:T(8,128)S(1)}, u32[]{:S(2)}, u32[]{:S(2)}) collective-permute-start(f32[4,32,2048]{2,1,0:T(8,128)S(1)} %get-tuple-element.25), channel_id=1, source_target_pairs={{1,0},{2,1},{3,2},{0,3},{5,4},{6,5},{7,6},{4,7},{9,8},{10,9},{11,1... | collective-permute-start | bytes 3145736 | tf_op jit(solution)/shard_map/ppermute | solution.py:457
  15.3 56.5 %collective-permute-start = (f32[4,32,2048]{2,1,0:T(8,128)S(1)}, f32[4,32,2048]{2,1,0:T(8,128)S(1)}, u32[]{:S(2)}, u32[]{:S(2)}) collective-permute-start(f32[4,32,2048]{2,1,0:T(8,128)S(1)} %get-tuple-element.23), channel_id=1, source_target_pairs={{0,1},{1,2},{2,3},{4,5},{5,6},{6,7},{8,9},{9,10},{10,11},{12,13},{... | collective-permute-start | bytes 3145736 | tf_op jit(solution)/shard_map/ppermute | solution.py:482
  66.3 5.4 %collective-permute-start.3 = (f32[8,128]{1,0:T(8,128)S(1)}, f32[8,128]{1,0:T(8,128)S(1)}, u32[]{:S(2)}, u32[]{:S(2)}) collective-permute-start(f32[8,128]{1,0:T(8,128)S(1)} %get-tuple-element.35), channel_id=1, source_target_pairs={{0,1},{1,2},{2,3},{3,0},{4,5},{5,6},{6,7},{7,4},{8,9},{9,10},{10,1... | collective-permute-start | bytes 12296 | tf_op jit(solution)/shard_map/ppermute | solution.py:511

commit v3 on v2

--- a/solution.py
+++ b/solution.py
@@ -82,12 +82,11 @@
     return out, carried
 
 
-def load(x_hbm, near, head, x_ref, sems):
+def cut(x_hbm, near, head, sems):
     rows = x_hbm.shape[1]
     copies = [
         pltpu.make_async_copy(x_hbm.at[:, pl.ds(rows - LATE, LATE), :], near, sems.at[0]),
         pltpu.make_async_copy(x_hbm.at[:, pl.ds(0, LATE), :], head, sems.at[1]),
-        pltpu.make_async_copy(x_hbm, x_ref, sems.at[2]),
     ]
     for copy in copies:
         copy.start()
@@ -95,44 +94,63 @@
         copy.wait()
 
 
-def first_pass(
-    x_ref, from_hbm, until_hbm,
-    buf, inverse, pay, far, from_ref, until_ref, sums, counts, date_sems,
-):
+def load(x_hbm, from_hbm, until_hbm, x_ref, inverse, tally, from_ref, until_ref, sems):
+    fields, rows, assets = x_hbm.shape
+    own_groups = rows // GROUP
+    groups = own_groups + LATE_GROUPS
+    main = own_groups - SKIP_GROUPS
+    base, base_next = block_starts(rows)
+    dates = [
+        pltpu.make_async_copy(from_hbm, from_ref, sems.at[0]),
+        pltpu.make_async_copy(until_hbm, until_ref, sems.at[1]),
+    ]
+    whole = pltpu.make_async_copy(x_hbm, x_ref, sems.at[2])
+    for copy in dates:
+        copy.start()
+    whole.start()
+    width = 4 * LANE
+    sub = sublanes(width)
+    for copy in dates:
+        copy.wait()
+    lane = lanes_iota()
+    first = fields * main
+    tiles = [jnp.zeros((GROUP, LANE), jnp.float32) for _ in range(2)]
+    for g in range(groups):
+        at = base + g * GROUP if g < own_groups else base_next + (g - own_groups) * GROUP
+        count = jnp.zeros((GROUP, LANE), jnp.float32)
+        for start in range(0, assets, width):
+            lanes = pl.ds(start, width)
+            seen = sub - jnp.maximum(from_ref[:, lanes], 0) + at
+            listed = (seen >= 0) & (until_ref[:, lanes] - sub > at)
+            counted = jnp.clip(seen + 1, 1, WINDOW).astype(jnp.float32)
+            inverse[rows_of(g), lanes] = jnp.where(listed, 1.0 / counted, 0.0)
+            count = count + folded(jnp.where(listed, 1.0, 0.0))
+        if SKIP_GROUPS <= g < own_groups:
+            tiles[0] = jnp.where(lane == first + g - SKIP_GROUPS, total_of(count), tiles[0])
+        elif g >= SKIP_GROUPS - LATE_GROUPS:
+            side = 0 if g < SKIP_GROUPS else 1
+            k = g - LATE_GROUPS if side == 0 else g - own_groups
+            spot = lane - (first + side * fields * LATE_GROUPS)
+            here = (spot >= 0) & (spot < fields * LATE_GROUPS) & (lax.rem(spot, LATE_GROUPS) == k)
+            tiles[1] = jnp.where(here, total_of(count), tiles[1])
+    tally[:GROUP, :] = tiles[0]
+    tally[GROUP:, :] = tiles[1]
+    whole.wait()
+
+
+def first_pass(x_ref, from_ref, inverse, tally, buf, pay, far, sums):
     fields, rows, assets = x_ref.shape
     own_groups = rows // GROUP
     groups = own_groups + LATE_GROUPS
     main = own_groups - SKIP_GROUPS
     width = 2 * LANE
-    base, base_next = block_starts(rows)
-    dates = [
-        pltpu.make_async_copy(from_hbm, from_ref, date_sems.at[0]),
-        pltpu.make_async_copy(until_hbm, until_ref, date_sems.at[1]),
-    ]
-    for copy in dates:
-        copy.start()
+    base = block_starts(rows)[0]
     sums[...] = jnp.zeros_like(sums)
-    counts[...] = jnp.zeros_like(counts)
     sub = sublanes(width)
-    for copy in dates:
-        copy.wait()
 
     def chunk(c, carry):
         lanes = pl.ds(pl.multiple_of(c * width, width), width)
-        opened = jnp.maximum(from_ref[:, lanes], 0)
-        closed = until_ref[:, lanes]
-        age = sub - opened
-        left = closed - sub
-        for g in range(groups):
-            at = base + g * GROUP if g < own_groups else base_next + (g - own_groups) * GROUP
-            seen = age + at
-            listed = (seen >= 0) & (left > at)
-            counted = jnp.clip(seen + 1, 1, WINDOW).astype(jnp.float32)
-            inverse[rows_of(g), lanes] = jnp.where(listed, 1.0 / counted, 0.0)
-            if g >= SKIP_GROUPS - LATE_GROUPS:
-                which = g - (SKIP_GROUPS - LATE_GROUPS)
-                counts[which] += folded(jnp.where(listed, 1.0, 0.0))
-        start = base + age
+        start = base + sub - jnp.maximum(from_ref[:, lanes], 0)
 
         def one_field(f, carry):
             last1 = last2 = last4 = last8 = None
@@ -172,20 +190,11 @@
 
     lax.fori_loop(0, assets // width, chunk, 0)
     lane = lanes_iota()
-    tiles = [jnp.zeros((GROUP, LANE), jnp.float32) for _ in range(2)]
+    tiles = [tally[:GROUP, :], tally[GROUP:, :]]
     for stat in range(2):
         for f in range(fields):
             for g in range(main):
                 tiles[stat] = jnp.where(lane == f * main + g, total_of(sums[stat, f, g]), tiles[stat])
-    first = fields * main
-    for g in range(main):
-        tiles[0] = jnp.where(lane == first + g, total_of(counts[LATE_GROUPS + g]), tiles[0])
-    for side in range(2):
-        for g in range(LATE_GROUPS):
-            spot = lane - (first + side * fields * LATE_GROUPS)
-            here = (spot >= 0) & (spot < fields * LATE_GROUPS) & (lax.rem(spot, LATE_GROUPS) == g)
-            at = g if side == 0 else LATE_GROUPS + main + g
-            tiles[1] = jnp.where(here, total_of(counts[at]), tiles[1])
     for d in range(pay.shape[0]):
         pay[d, :GROUP, :] = tiles[0]
         pay[d, GROUP:, :] = tiles[1]
@@ -330,27 +339,6 @@
         stage[f, put, lanes] = jnp.where(inverse[where, lanes] > 0.0, z, 0.0)
 
 
-def main_final_pass(buf, inverse, stats, level, out, stage, sems):
-    fields, rows, assets = out.shape
-    main = rows // GROUP - SKIP_GROUPS
-    width = 2 * LANE
-    c1, s1, c2, s2 = stats[0], stats[1], level[0], level[1]
-    copies = []
-    for f in range(fields):
-        for g in range(main):
-            spot = f * main + g
-            where = rows_of(g + SKIP_GROUPS)
-            cols = [column(t, spot, width) for t in (c1, s1, c2, s2)]
-            final_rows(f, where, buf, where, inverse, stage, rows_of(g), cols, assets)
-        copy = pltpu.make_async_copy(
-            stage.at[f], out.at[f, pl.ds(WINDOW, rows - WINDOW), :], sems.at[f]
-        )
-        copy.start()
-        copies.append(copy)
-    for copy in copies:
-        copy.wait()
-
-
 def send_pass(gathered, stats, level, level4, pay):
     total = summed(gathered)
     back = 32
@@ -365,37 +353,37 @@
     pay[...] = out
 
 
-def late_final_pass(late, inverse, level, level4, prior, out, stage, sems):
-    fields, _, assets = late.shape
-    width = 2 * LANE
+def final_pass(
+    buf, late, tail, whole, from_ref, inverse, stats, level, level4,
+    out, rolled, stage, sems,
+):
+    fields, rows, assets = out.shape
+    main = rows // GROUP - SKIP_GROUPS
     first = LANE - 2 * fields * LATE_GROUPS
+    width = 2 * LANE
+    late_tiles = (level[0], level[1], level4[0], level4[1])
+    main_tiles = (stats[0], stats[1], level[0], level[1])
     copies = []
     for f in range(fields):
         for g in range(LATE_GROUPS):
             spot = first + f * LATE_GROUPS + g
-            tiles = (level[0], level[1], level4[0], level4[1])
-            cols = [column(t, spot, width) for t in tiles]
+            cols = [column(t, spot, width) for t in late_tiles]
             where = rows_of(LATE_GROUPS + g)
             final_rows(f, where, late, rows_of(g), inverse, stage, rows_of(g), cols, assets)
-        copy = pltpu.make_async_copy(stage.at[f], out.at[f, pl.ds(LATE, LATE), :], sems.at[f])
+        for g in range(main):
+            cols = [column(t, f * main + g, width) for t in main_tiles]
+            where = rows_of(g + SKIP_GROUPS)
+            put = rows_of(LATE_GROUPS + g)
+            final_rows(f, where, buf, where, inverse, stage, put, cols, assets)
+        copy = pltpu.make_async_copy(
+            stage.at[f], out.at[f, pl.ds(LATE, rows - LATE), :], sems.at[f]
+        )
         copy.start()
         copies.append(copy)
-    for copy in copies:
-        copy.wait()
-
-
-def head_final_pass(buf, tail, whole, from_ref, inverse, sent, prior, out, stage, sems):
-    fields, _, assets = buf.shape
-    base = block_starts(inverse.shape[0] - LATE)[0]
+    base = block_starts(rows)[0]
     width = 4 * LANE
     sub = sublanes(width)
-    levels = sent[...]
-    copies = []
     for f in range(fields):
-        cols = [
-            [column(levels, 16 * i + f * LATE_GROUPS + g, width) for i in range(4)]
-            for g in range(LATE_GROUPS)
-        ]
 
         def tile(i, carry):
             lanes = pl.ds(pl.multiple_of(i * width, width), width)
@@ -407,14 +395,25 @@
             running, last = prefix_groups(masked, width)
             last = last + whole[f, :, lanes]
             for g in range(LATE_GROUPS):
-                c1, s1, c2, s2 = cols[g]
-                weight = inverse[rows_of(g), lanes]
-                r = (buf[f, rows_of(g), lanes] + (last - running[g])) * weight
-                z = (clipped_score(r, c1, s1) - c2) * s2
-                stage[f, rows_of(g), lanes] = jnp.where(weight > 0.0, z, 0.0)
+                r = buf[f, rows_of(g), lanes] + (last - running[g])
+                rolled[f, rows_of(g), lanes] = r * inverse[rows_of(g), lanes]
             return carry
 
         lax.fori_loop(0, assets // width, tile, 0)
+    for copy in copies:
+        copy.wait()
+
+
+def head_final_pass(rolled, inverse, sent, prior, out, stage, sems):
+    fields, _, assets = rolled.shape
+    width = 2 * LANE
+    levels = sent[...]
+    copies = []
+    for f in range(fields):
+        for g in range(LATE_GROUPS):
+            cols = [column(levels, 16 * i + f * LATE_GROUPS + g, width) for i in range(4)]
+            rows = rows_of(g)
+            final_rows(f, rows, rolled, rows, inverse, stage, rows, cols, assets)
         copy = pltpu.make_async_copy(stage.at[f], out.at[f, pl.ds(0, LATE), :], sems.at[f])
         copy.start()
         copies.append(copy)
@@ -444,16 +443,15 @@
     fields, rows, assets = values.shape
     n = lax.axis_size("asset")
     blocks = lax.axis_size("tm")
-    forward = [(i, i + 1) for i in range(blocks - 1)]
     ring = [(i, (i + 1) % blocks) for i in range(blocks)]
     back = [((i + 1) % blocks, i) for i in range(blocks)]
     work = fields * rows * assets
     slab = shape(fields, LATE, assets)
-    near, head, held = call(
-        load, "load", [HBM], (slab, slab, shape(fields, rows, assets)), (VMEM,) * 3,
-        [pltpu.SemaphoreType.DMA((3,))], limit=40, flops=work // 8,
+    near, head = call(
+        cut, "cut", [HBM], (slab, slab), (VMEM, VMEM), [pltpu.SemaphoreType.DMA((2,))],
+        limit=50,
     )(values)
-    tail_near = lax.ppermute(near, "tm", forward)
+    tail_near = lax.ppermute(near, "tm", ring)
     head = lax.ppermute(head, "tm", back)
     opened, closed = listed_from.reshape(1, assets), listed_until.reshape(1, assets)
     main = rows // GROUP - SKIP_GROUPS
@@ -463,23 +461,24 @@
         lax.all_to_all, axis_name="asset", split_axis=0, concat_axis=0, tiled=True
     )
 
-    buf, inverse, pay, far = call(
-        first_pass, "first_pass", [VMEM, HBM, HBM],
-        (
-            shape(fields, rows + LATE, assets), shape(rows + LATE, assets),
-            shape(n, 2 * GROUP, LANE), slab,
-        ),
-        (VMEM,) * 4,
+    held, inverse, tally = call(
+        load, "load", [HBM] * 3,
+        (shape(fields, rows, assets), shape(rows + LATE, assets), shape(2 * GROUP, LANE)),
+        (VMEM,) * 3,
         [
             pltpu.VMEM((1, assets), jnp.int32),
             pltpu.VMEM((1, assets), jnp.int32),
-            pltpu.VMEM((2, fields, main, GROUP, LANE), jnp.float32),
-            pltpu.VMEM((main + 2 * LATE_GROUPS, GROUP, LANE), jnp.float32),
-            pltpu.SemaphoreType.DMA((2,)),
+            pltpu.SemaphoreType.DMA((3,)),
         ],
-        limit=8, flops=20 * work,
-    )(held, opened, closed)
-    tail_far = lax.ppermute(far, "tm", forward)
+        limit=40, flops=work,
+    )(values, opened, closed)
+    buf, pay, far = call(
+        first_pass, "first_pass", [VMEM] * 4,
+        (shape(fields, rows + LATE, assets), shape(n, 2 * GROUP, LANE), slab),
+        (VMEM,) * 3,
+        [pltpu.VMEM((2, fields, main, GROUP, LANE), jnp.float32)], flops=20 * work,
+    )(held, opened, inverse, tally)
+    tail_far = lax.ppermute(far, "tm", ring)
     gathered = exchange(pay)
     stats, part = call(
         second_pass, "second_pass", [VMEM] * 3,
@@ -496,31 +495,25 @@
         (pair, shape(n, GROUP, LANE)), (VMEM, VMEM), limit=16, flops=3 * work,
     )(gathered, stats, late, inverse)
     gathered = exchange(pay)
-    out = call(
-        main_final_pass, "main_final_pass", [VMEM] * 4,
-        shape(fields, rows, assets), HBM,
-        [
-            pltpu.VMEM((fields, rows - WINDOW, assets), jnp.float32),
-            pltpu.SemaphoreType.DMA((fields,)),
-        ],
-        limit=20, flops=10 * work,
-    )(buf, inverse, stats, level)
     level4, pay = call(
         send_pass, "send_pass", [VMEM] * 3, (pair, tile), (VMEM, VMEM), flops=work // 100,
     )(gathered, stats, level)
     sent = lax.ppermute(pay, "tm", ring)
-    stage = [
-        pltpu.VMEM((fields, LATE, assets), jnp.float32),
-        pltpu.SemaphoreType.DMA((fields,)),
-    ]
-    out = call(
-        late_final_pass, "late_final_pass", [VMEM] * 4 + [HBM],
-        shape(fields, rows, assets), HBM, stage, limit=16, flops=2 * work, aliases={4: 0},
-    )(late, inverse, level, level4, out)
+    out, rolled = call(
+        final_pass, "final_pass", [VMEM] * 9,
+        (shape(fields, rows, assets), slab), (HBM, VMEM),
+        [
+            pltpu.VMEM((fields, rows - LATE, assets), jnp.float32),
+            pltpu.SemaphoreType.DMA((fields,)),
+        ],
+        limit=16, flops=10 * work,
+    )(buf, late, tail_far, whole, opened, inverse, stats, level, level4)
     return call(
-        head_final_pass, "head_final_pass", [VMEM] * 6 + [HBM],
-        shape(fields, rows, assets), HBM, stage, limit=16, flops=2 * work, aliases={6: 0},
-    )(buf, tail_far, whole, opened, inverse, sent, out)
+        head_final_pass, "head_final_pass", [VMEM] * 3 + [HBM],
+        shape(fields, rows, assets), HBM,
+        [pltpu.VMEM((fields, LATE, assets), jnp.float32), pltpu.SemaphoreType.DMA((fields,))],
+        limit=16, flops=2 * work, aliases={3: 0},
+    )(rolled, inverse, sent, out)
 
 
 def solution(mesh):

time: 74 us -> 68.4 us (0.924)
  starting transfers between devices: 8.63 us -> 4.88 us
  Pallas kernels: 23.1 us -> 21.2 us
    ppermute x2, starting transfers between devices: 6.85 us -> 2.28 us  [the longest x1 2.1 us: per_device(): tail_near = lax.ppermute(near, 'tm', ring)]
    pallas_call x5, Pallas kernels: 16.9 us -> 15 us  [the longest x1 5.34 us: per_device(): call(first_pass, 'first_pass', [VMEM] * 4, (shape(fields, rows + LATE, as...]
  transfers between devices with their start and end apart: 4 -> 4, of which waited for: 0 -> 0; matrix products, arithmetic and copies ran while one was open for 0% -> 0% of each run, Pallas kernels for 23% -> 27%
where the time goes in v3:
time: 68.4 us; the launch traced here: 68.1 us
  blocking collectives  41.9 us (61%)
  Pallas kernels  21.2 us (31%)
  starting transfers between devices  4.88 us (7%)
    all_to_all x3, blocking collectives, per_device(): gathered = exchange(pay)  41.9 us
    pallas_call x1, Pallas kernels, per_device(): call(first_pass, 'first_pass', [VMEM] * 4, (shape(fields, rows + LATE, as...  5.34 us
    pallas_call x1, Pallas kernels, per_device(): call(final_pass, 'final_pass', [VMEM] * 9, (shape(fields, rows, assets),...  3.56 us
    pallas_call x1, Pallas kernels, per_device(): call(load, 'load', [HBM] * 3, (shape(fields, rows, assets), shape(rows +...  3.42 us
    pallas_call x1, Pallas kernels, per_device(): call(second_pass, 'second_pass', [VMEM] * 3, (shape(3, GROUP, LANE), shap...  3.22 us
    ppermute x1, starting transfers between devices, per_device(): tail_near = lax.ppermute(near, 'tm', ring)  2.1 us
    pallas_call x1, Pallas kernels, per_device(): call(late_first_pass, 'late_first_pass', [VMEM] * 6, (shape(fields, 2 * L...  1.83 us
    pallas_call x1, Pallas kernels, per_device(): call(cut, 'cut', [HBM], (slab, slab), (VMEM, VMEM), [pltpu.SemaphoreType....  1.58 us
  transfers between devices with their start and end apart: 4, of which 0 were waited for; matrix products, arithmetic and copies ran while one was open for 0% of the time, Pallas kernels for 27%

profile of v3, /device:TPU:1, one launch (start us, length us, event | category | flops | bytes accessed | tf_op | source)
XLA Modules:
  0.0 68.1 jit_solution(1868762799322239319)
XLA Ops:
  0.0 0.0 copy-start.1
  0.0 0.0 copy-start
  0.0 1.6 %cut.1 = (f32[4,32,2048]{2,1,0:T(8,128)S(1)}, f32[4,32,2048]{2,1,0:T(8,128)S(1)}) custom-call(f32[4,256,2048]{2,1,0:T(8,128)} %x_hbm.3), custom_call_target="tpu_custom_call" | custom-call | tf_op jit(solution)/shard_map/cut/pallas_call | solution.py:450
  1.6 2.1 %collective-permute-start = (f32[4,32,2048]{2,1,0:T(8,128)S(1)}, f32[4,32,2048]{2,1,0:T(8,128)S(1)}, u32[]{:S(2)}, u32[]{:S(2)}) collective-permute-start(f32[4,32,2048]{2,1,0:T(8,128)S(1)} %get-tuple-element.28), channel_id=1, source_target_pairs={{0,1},{1,2},{2,3},{3,0},{4,5},{5,6},{6,7},{7,4},{8,9},{9,10},{10,1... | collective-permute-start | bytes 3145736 | tf_op jit(solution)/shard_map/ppermute | solution.py:454
  3.7 1.3 %collective-permute-start.1 = (f32[4,32,2048]{2,1,0:T(8,128)S(1)}, f32[4,32,2048]{2,1,0:T(8,128)S(1)}, u32[]{:S(2)}, u32[]{:S(2)}) collective-permute-start(f32[4,32,2048]{2,1,0:T(8,128)S(1)} %get-tuple-element.29), channel_id=1, source_target_pairs={{1,0},{2,1},{3,2},{0,3},{5,4},{6,5},{7,6},{4,7},{9,8},{10,9},{11,1... | collective-permute-start | bytes 3145736 | tf_op jit(solution)/shard_map/ppermute | solution.py:455
  5.0 0.0 copy-done.1
  5.0 0.0 copy-done
  5.0 3.4 %load.1 = (f32[4,256,2048]{2,1,0:T(8,128)S(1)}, f32[288,2048]{1,0:T(8,128)S(1)}, f32[16,128]{1,0:T(8,128)S(1)}) custom-call(f32[4,256,2048]{2,1,0:T(8,128)} %x_hbm.3, s32[1,2048]{1,0:T(1,128)S(1)} %bitcast.2, s32[1,2048]{1,0:T(1,128)S(1)} %bitcast.6), custom_call_target="tpu_custom_call" | custom-call | flops 2097152 | tf_op jit(solution)/shard_map/load/pallas_call | solution.py:464
  8.5 5.3 %first_pass.1 = (f32[4,288,2048]{2,1,0:T(8,128)S(1)}, f32[32,16,128]{2,1,0:T(8,128)S(1)}, f32[4,32,2048]{2,1,0:T(8,128)S(1)}) custom-call(f32[4,256,2048]{2,1,0:T(8,128)S(1)} %get-tuple-element.24.x_ref, s32[1,2048]{1,0:T(1,128)S(1)} %bitcast.3, f32[288,2048]{1,0:T(8,128)S(1)} %get-tuple-element.25.inverse, f32[16,128]{1,0:T(8,128)S(1)} %get-tuple-element.26.tally), custom_call_target="tpu_custom_call" | custom-call | flops 41943040 | tf_op jit(solution)/shard_map/first_pass/pallas_call | solution.py:475
  13.8 0.2 collective-permute-start.2
  14.0 18.4 %all_to_all.15.gathered = f32[32,16,128]{2,1,0:T(8,128)S(1)} all-to-all(f32[32,16,128]{2,1,0:T(8,128)S(1)} %get-tuple-element.30), channel_id=1, replica_groups=mesh['asset'=32,'tm'=4] {'asset'}, dimensions={0} | all-to-all | bytes 524288 | tf_op jit(solution)/shard_map/all_to_all | solution.py:482
  32.4 3.2 %second_pass.1 = (f32[3,8,128]{2,1,0:T(8,128)S(1)}, f32[16,128]{1,0:T(8,128)S(1)}) custom-call(f32[32,16,128]{2,1,0:T(8,128)S(1)} %all_to_all.15.gathered, f32[4,288,2048]{2,1,0:T(8,128)S(1)} %get-tuple-element.27.buf, f32[288,2048]{1,0:T(8,128)S(1)} %get-tuple-element.25.inverse), custom_call_target="tpu_custom_call" | custom-call | flops 20971520 | tf_op jit(solution)/shard_map/second_pass/pallas_call | solution.py:483
  35.6 0.0 collective-permute-done.tail
  35.6 0.0 collective-permute-done.1.head
  35.6 1.8 %late_first_pass.1 = (f32[4,64,2048]{2,1,0:T(8,128)S(1)}, f32[4,8,2048]{2,1,0:T(8,128)S(1)}, f32[32,16,128]{2,1,0:T(8,128)S(1)}) custom-call(f32[4,288,2048]{2,1,0:T(8,128)S(1)} %get-tuple-element.27.buf, f32[4,32,2048]{2,1,0:T(8,128)S(1)} %collective-permute-done.tail, f32[4,32,2048]{2,1,0:T(8,128)S(1)} %collective-permute-done.1.head, ...), custom_call_target="tpu_custom_call" | custom-call | flops 10485760 | tf_op jit(solution)/shard_map/late_first_pass/pallas_call | solution.py:487
  37.4 12.4 %all_to_all.16.gathered = f32[32,16,128]{2,1,0:T(8,128)S(1)} all-to-all(f32[32,16,128]{2,1,0:T(8,128)S(1)} %get-tuple-element.36), channel_id=1, replica_groups=mesh['asset'=32,'tm'=4] {'asset'}, dimensions={0} | all-to-all | bytes 524288 | tf_op jit(solution)/shard_map/all_to_all | solution.py:492
  49.9 1.0 %late_second_pass.1 = (f32[2,8,128]{2,1,0:T(8,128)S(1)}, f32[32,8,128]{2,1,0:T(8,128)S(1)}) custom-call(f32[32,16,128]{2,1,0:T(8,128)S(1)} %all_to_all.16.gathered, f32[3,8,128]{2,1,0:T(8,128)S(1)} %get-tuple-element.35.stats, f32[4,64,2048]{2,1,0:T(8,128)S(1)} %get-tuple-element.32.late, f32[288,2048]{1,0:T(8,128)S(1)} %get-tuple-element.25.inverse), custom_call_target="tpu_custom_call" | custom-call | flops 6291456 | tf_op jit(solution)/shard_map/late_second_pass/pallas_call | solution.py:493
  50.8 11.1 %all_to_all.17.gathered = f32[32,8,128]{2,1,0:T(8,128)S(1)} all-to-all(f32[32,8,128]{2,1,0:T(8,128)S(1)} %get-tuple-element.38), channel_id=1, replica_groups=mesh['asset'=32,'tm'=4] {'asset'}, dimensions={0} | all-to-all | bytes 262144 | tf_op jit(solution)/shard_map/all_to_all | solution.py:497
  62.0 0.1 send_pass.1
  62.1 1.2 %collective-permute-start.3 = (f32[8,128]{1,0:T(8,128)S(1)}, f32[8,128]{1,0:T(8,128)S(1)}, u32[]{:S(2)}, u32[]{:S(2)}) collective-permute-start(f32[8,128]{1,0:T(8,128)S(1)} %get-tuple-element.41), channel_id=1, source_target_pairs={{0,1},{1,2},{2,3},{3,0},{4,5},{5,6},{6,7},{7,4},{8,9},{9,10},{10,1... | collective-permute-start | bytes 12296 | tf_op jit(solution)/shard_map/ppermute | solution.py:501
  63.4 0.0 collective-permute-done.2.tail
  63.4 3.6 %final_pass.1 = (f32[4,256,2048]{2,1,0:T(8,128)}, f32[4,32,2048]{2,1,0:T(8,128)S(1)}) custom-call(f32[4,288,2048]{2,1,0:T(8,128)S(1)} %get-tuple-element.27.buf, f32[4,64,2048]{2,1,0:T(8,128)S(1)} %get-tuple-element.32.late, f32[4,32,2048]{2,1,0:T(8,128)S(1)} %collective-permute-done.2.tail, f32[4,8,2048]{2,1,0:T(8,128)S(1)} %get-tuple-element.34.whole, ...), custom_call_target="tpu_custom_call" | custom-call | flops 20971520 | tf_op jit(solution)/shard_map/final_pass/pallas_call | solution.py:502
  66.9 0.0 collective-permute-done.3.sent
  67.0 1.1 %head_final_pass.1 = f32[4,256,2048]{2,1,0:T(8,128)} custom-call(f32[4,32,2048]{2,1,0:T(8,128)S(1)} %get-tuple-element.40.rolled, f32[288,2048]{1,0:T(8,128)S(1)} %get-tuple-element.25.inverse, f32[8,128]{1,0:T(8,128)S(1)} %collective-permute-done.3.sent, f32[4,256,2048]{2,1,0:T(8,128)} %get-tuple-element.42.prior), custom_call_target="tpu_custom_call", output_to_operand_aliasing={{}: (3, {})} | custom-call | flops 4194304 | tf_op jit(solution)/shard_map/head_final_pass/pallas_call | solution.py:511
Async XLA Ops:
  0.0 5.0 %copy-start.1 = (s32[2048]{0:T(1024)S(1)}, s32[2048]{0:T(1024)}, u32[]{:S(2)}) copy-start(s32[2048]{0:T(1024)} %param.5) | copy-start | bytes 24580
  0.0 5.0 %copy-start = (s32[2048]{0:T(1024)S(1)}, s32[2048]{0:T(1024)}, u32[]{:S(2)}) copy-start(s32[2048]{0:T(1024)} %param.4) | copy-start | bytes 24580
  1.6 34.0 %collective-permute-start = (f32[4,32,2048]{2,1,0:T(8,128)S(1)}, f32[4,32,2048]{2,1,0:T(8,128)S(1)}, u32[]{:S(2)}, u32[]{:S(2)}) collective-permute-start(f32[4,32,2048]{2,1,0:T(8,128)S(1)} %get-tuple-element.28), channel_id=1, source_target_pairs={{0,1},{1,2},{2,3},{3,0},{4,5},{5,6},{6,7},{7,4},{8,9},{9,10},{10,1... | collective-permute-start | bytes 3145736 | tf_op jit(solution)/shard_map/ppermute | solution.py:454
  3.7 31.9 %collective-permute-start.1 = (f32[4,32,2048]{2,1,0:T(8,128)S(1)}, f32[4,32,2048]{2,1,0:T(8,128)S(1)}, u32[]{:S(2)}, u32[]{:S(2)}) collective-permute-start(f32[4,32,2048]{2,1,0:T(8,128)S(1)} %get-tuple-element.29), channel_id=1, source_target_pairs={{1,0},{2,1},{3,2},{0,3},{5,4},{6,5},{7,6},{4,7},{9,8},{10,9},{11,1... | collective-permute-start | bytes 3145736 | tf_op jit(solution)/shard_map/ppermute | solution.py:455
  13.8 49.6 %collective-permute-start.2 = (f32[4,32,2048]{2,1,0:T(8,128)S(1)}, f32[4,32,2048]{2,1,0:T(8,128)S(1)}, u32[]{:S(2)}, u32[]{:S(2)}) collective-permute-start(f32[4,32,2048]{2,1,0:T(8,128)S(1)} %get-tuple-element.33), channel_id=1, source_target_pairs={{0,1},{1,2},{2,3},{3,0},{4,5},{5,6},{6,7},{7,4},{8,9},{9,10},{10,1... | collective-permute-start | bytes 3145736 | tf_op jit(solution)/shard_map/ppermute | solution.py:481
  62.1 4.8 %collective-permute-start.3 = (f32[8,128]{1,0:T(8,128)S(1)}, f32[8,128]{1,0:T(8,128)S(1)}, u32[]{:S(2)}, u32[]{:S(2)}) collective-permute-start(f32[8,128]{1,0:T(8,128)S(1)} %get-tuple-element.41), channel_id=1, source_target_pairs={{0,1},{1,2},{2,3},{3,0},{4,5},{5,6},{6,7},{7,4},{8,9},{9,10},{10,1... | collective-permute-start | bytes 12296 | tf_op jit(solution)/shard_map/ppermute | solution.py:501

commit v4 on v3

--- a/solution.py
+++ b/solution.py
@@ -94,32 +94,42 @@
         copy.wait()
 
 
-def load(x_hbm, from_hbm, until_hbm, x_ref, inverse, tally, from_ref, until_ref, sems):
+def first_pass(
+    x_hbm, from_hbm, until_hbm,
+    edge, low, high, inverse, pay, far, from_ref, until_ref, xs, sums, sems, date_sems,
+):
     fields, rows, assets = x_hbm.shape
     own_groups = rows // GROUP
     groups = own_groups + LATE_GROUPS
     main = own_groups - SKIP_GROUPS
     base, base_next = block_starts(rows)
+    chunks, _, _, width = xs.shape
+
+    def fetch(c):
+        lanes = pl.ds(pl.multiple_of(c * width, width), width)
+        return pltpu.make_async_copy(x_hbm.at[:, :, lanes], xs.at[c], sems.at[c])
+
     dates = [
-        pltpu.make_async_copy(from_hbm, from_ref, sems.at[0]),
-        pltpu.make_async_copy(until_hbm, until_ref, sems.at[1]),
+        pltpu.make_async_copy(from_hbm, from_ref, date_sems.at[0]),
+        pltpu.make_async_copy(until_hbm, until_ref, date_sems.at[1]),
     ]
-    whole = pltpu.make_async_copy(x_hbm, x_ref, sems.at[2])
     for copy in dates:
         copy.start()
-    whole.start()
-    width = 4 * LANE
-    sub = sublanes(width)
-    for copy in dates:
-        copy.wait()
+    for c in range(chunks):
+        fetch(c).start()
+    sums[...] = jnp.zeros_like(sums)
+    wide = 4 * LANE
+    sub = sublanes(wide)
     lane = lanes_iota()
     first = fields * main
     tiles = [jnp.zeros((GROUP, LANE), jnp.float32) for _ in range(2)]
+    for copy in dates:
+        copy.wait()
     for g in range(groups):
         at = base + g * GROUP if g < own_groups else base_next + (g - own_groups) * GROUP
         count = jnp.zeros((GROUP, LANE), jnp.float32)
-        for start in range(0, assets, width):
-            lanes = pl.ds(start, width)
+        for start in range(0, assets, wide):
+            lanes = pl.ds(start, wide)
             seen = sub - jnp.maximum(from_ref[:, lanes], 0) + at
             listed = (seen >= 0) & (until_ref[:, lanes] - sub > at)
             counted = jnp.clip(seen + 1, 1, WINDOW).astype(jnp.float32)
@@ -133,24 +143,12 @@
             spot = lane - (first + side * fields * LATE_GROUPS)
             here = (spot >= 0) & (spot < fields * LATE_GROUPS) & (lax.rem(spot, LATE_GROUPS) == k)
             tiles[1] = jnp.where(here, total_of(count), tiles[1])
-    tally[:GROUP, :] = tiles[0]
-    tally[GROUP:, :] = tiles[1]
-    whole.wait()
-
-
-def first_pass(x_ref, from_ref, inverse, tally, buf, pay, far, sums):
-    fields, rows, assets = x_ref.shape
-    own_groups = rows // GROUP
-    groups = own_groups + LATE_GROUPS
-    main = own_groups - SKIP_GROUPS
-    width = 2 * LANE
-    base = block_starts(rows)[0]
-    sums[...] = jnp.zeros_like(sums)
     sub = sublanes(width)
 
     def chunk(c, carry):
         lanes = pl.ds(pl.multiple_of(c * width, width), width)
         start = base + sub - jnp.maximum(from_ref[:, lanes], 0)
+        fetch(c).wait()
 
         def one_field(f, carry):
             last1 = last2 = last4 = last8 = None
@@ -158,9 +156,9 @@
             for g in range(groups):
                 if own_groups - SKIP_GROUPS <= g < own_groups - LATE_GROUPS:
                     to = rows_of(g - (own_groups - SKIP_GROUPS))
-                    far[f, to, lanes] = x_ref[f, rows_of(g), lanes]
+                    far[f, to, lanes] = xs[c, f, rows_of(g), :]
                 if g < own_groups:
-                    x = jnp.where(start >= -g * GROUP, x_ref[f, rows_of(g), lanes], 0.0)
+                    x = jnp.where(start >= -g * GROUP, xs[c, f, rows_of(g), :], 0.0)
                 else:
                     x = jnp.zeros((GROUP, width), jnp.float32)
                 r = pltpu.roll(x, 1, 0)
@@ -182,15 +180,17 @@
                     x64 = x64 * inverse[rows_of(g), lanes]
                     sums[0, f, g - SKIP_GROUPS] += folded(x64)
                     sums[1, f, g - SKIP_GROUPS] += folded(x64 * x64)
-                buf[f, rows_of(g), lanes] = x64
+                    to, at = divmod(g - SKIP_GROUPS, main // 2)
+                    (low, high)[to][f, rows_of(at), lanes] = x64
+                else:
+                    to = g if g < SKIP_GROUPS else g - main
+                    edge[f, rows_of(to), lanes] = x64
             return carry
 
         lax.fori_loop(0, fields, one_field, 0)
         return carry
 
-    lax.fori_loop(0, assets // width, chunk, 0)
-    lane = lanes_iota()
-    tiles = [tally[:GROUP, :], tally[GROUP:, :]]
+    lax.fori_loop(0, chunks, chunk, 0)
     for stat in range(2):
         for f in range(fields):
             for g in range(main):
@@ -200,27 +200,38 @@
         pay[d, GROUP:, :] = tiles[1]
 
 
+def spread_columns(tile, cols, spots):
+    for i, spot in enumerate(spots):
+        cols[i] = column(tile, spot, LANE)
+
+
+def tiles_of(assets):
+    return [pl.ds(at, LANE) for at in range(0, assets, LANE)]
+
+
 def row_moments(source, mine, inverse, where, cs, ss):
     fields, _, assets = source.shape
-    width = 2 * LANE
     acc = [None] * (2 * fields)
 
     def added(i, x):
         acc[i] = x if acc[i] is None else acc[i] + x
 
-    for at in range(0, assets, width):
-        lanes = pl.ds(at, width)
+    for lanes in tiles_of(assets):
         listed = inverse[where, lanes] > 0.0
         for f in range(fields):
             z = clipped_score(source[f, mine, lanes], cs[f], ss[f])
             z = jnp.where(listed, z, 0.0)
-            added(f, folded(z))
-            added(fields + f, folded(z * z))
+            added(f, z)
+            added(fields + f, z * z)
     return acc
 
 
-def second_pass(gathered, buf, inverse, stats, part):
-    fields, _, assets = buf.shape
+def group_rows(g):
+    return pl.ds(pl.multiple_of(g * GROUP, GROUP), GROUP)
+
+
+def second_pass(gathered, low, high, inverse, stats, part, centers, scales, sums):
+    fields, _, assets = low.shape
     main = (inverse.shape[0] - LATE) // GROUP - SKIP_GROUPS
     first = fields * main
     total = summed(gathered)
@@ -233,25 +244,33 @@
     present = jnp.maximum(present, 1.0)
     center, scale = moments(t0, t1, present)
     stats[0], stats[1], stats[2] = center, scale, present
-    width = 2 * LANE
-    tiles = [jnp.zeros((GROUP, LANE), jnp.float32) for _ in range(2)]
-    for g in range(main):
-        rows = rows_of(g + SKIP_GROUPS)
-        cs = [column(center, f * main + g, width) for f in range(fields)]
-        ss = [column(scale, f * main + g, width) for f in range(fields)]
-
-        acc = row_moments(buf, rows, inverse, rows, cs, ss)
-        for f in range(fields):
+    spread_columns(center, centers, range(first))
+    spread_columns(scale, scales, range(first))
+
+    half = main // 2
+    for source, skip in ((low, 0), (high, half)):
+
+        def group(i, carry):
+            g = i + skip
+            cs = [centers[f * main + g] for f in range(fields)]
+            ss = [scales[f * main + g] for f in range(fields)]
+            where = group_rows(g + SKIP_GROUPS)
+            acc = row_moments(source, group_rows(i), inverse, where, cs, ss)
             for stat in range(2):
-                tiles[stat] = jnp.where(
-                    lane == f * main + g, total_of(acc[stat * fields + f]), tiles[stat]
-                )
-    part[:GROUP, :] = tiles[0]
-    part[GROUP:, :] = tiles[1]
-
-
-def late_first_pass(buf, tail, head, from_ref, inverse, part, late, whole, pay):
-    fields, _, assets = buf.shape
+                for f in range(fields):
+                    sums[stat, f * main + g] = acc[stat * fields + f]
+            return carry
+
+        lax.fori_loop(0, half, group, 0)
+    for stat in range(2):
+        tile = jnp.zeros((GROUP, LANE), jnp.float32)
+        for spot in range(first):
+            tile = jnp.where(lane == spot, total_of(sums[stat, spot]), tile)
+        part[rows_of(stat), :] = tile
+
+
+def late_first_pass(edge, tail, head, from_ref, inverse, part, late, whole, pay):
+    fields, _, assets = edge.shape
     rows = inverse.shape[0] - LATE
     base, base_next = block_starts(rows)
     follows = jnp.where(base_next > 0, 1.0, 0.0)
@@ -278,10 +297,11 @@
                 for g in range(LATE_GROUPS):
                     if side == 0:
                         where = rows_of(LATE_GROUPS + g)
-                        r = buf[f, where, lanes] + (last - running[g])
+                        r = edge[f, where, lanes] + (last - running[g])
                     else:
                         where = rows_of(rows // GROUP + g)
-                        r = buf[f, where, lanes] * follows + running[g]
+                        start_rows = rows_of(SKIP_GROUPS + g)
+                        r = edge[f, start_rows, lanes] * follows + running[g]
                     r = r * inverse[where, lanes]
                     late[f, rows_of(side * LATE_GROUPS + g), lanes] = r
                     k = side * LATE_GROUPS + g
@@ -302,45 +322,52 @@
         pay[d, GROUP:, :] = tiles[1]
 
 
+def packed(t):
+    half = LANE // 2
+    low = pltpu.roll(t, half, 1)
+    lane = lax.broadcasted_iota(jnp.int32, (GROUP // 2, LANE), 1)
+    return jnp.where(lane < half, low[: GROUP // 2], t[GROUP // 2 :])
+
+
+def unpacked(p):
+    return jnp.concatenate([pltpu.roll(p, LANE // 2, 1), p], axis=0)
+
+
 def late_second_pass(gathered, stats, late, inverse, level, pay):
     fields, _, assets = late.shape
     rows = inverse.shape[0] - LATE
     total = summed(gathered)
     center, scale = moments(total[:GROUP], total[GROUP:], stats[2])
     level[0], level[1] = center, scale
-    width = 2 * LANE
     first = LANE - 2 * fields * LATE_GROUPS
+    back = LANE - first
     lane = lanes_iota()
     out = jnp.zeros((GROUP, LANE), jnp.float32)
     for side in range(2):
         for g in range(LATE_GROUPS):
             spots = [first + (side * fields + f) * LATE_GROUPS + g for f in range(fields)]
-            cs = [column(center, spot, width) for spot in spots]
-            ss = [column(scale, spot, width) for spot in spots]
+            cs = [column(center, spot, LANE) for spot in spots]
+            ss = [column(scale, spot, LANE) for spot in spots]
             where = rows_of(LATE_GROUPS + g if side == 0 else rows // GROUP + g)
             mine = rows_of(side * LATE_GROUPS + g)
-
             acc = row_moments(late, mine, inverse, where, cs, ss)
-            back = LANE - first
             for f in range(fields):
                 out = jnp.where(lane == spots[f], total_of(acc[f]), out)
                 out = jnp.where(lane == spots[f] - back, total_of(acc[fields + f]), out)
+    out = packed(out)
     for d in range(pay.shape[0]):
         pay[d] = out
 
 
-def final_rows(f, where, source, mine, inverse, stage, put, cols, assets):
-    width = 2 * LANE
+def final_rows(f, where, source, mine, inverse, stage, put, cols):
     c1, s1, c2, s2 = cols
-    for at in range(0, assets, width):
-        lanes = pl.ds(at, width)
-        z = clipped_score(source[f, mine, lanes], c1, s1)
-        z = (z - c2) * s2
+    for lanes in tiles_of(source.shape[2]):
+        z = (clipped_score(source[f, mine, lanes], c1, s1) - c2) * s2
         stage[f, put, lanes] = jnp.where(inverse[where, lanes] > 0.0, z, 0.0)
 
 
 def send_pass(gathered, stats, level, level4, pay):
-    total = summed(gathered)
+    total = unpacked(summed(gathered))
     back = 32
     square = pltpu.roll(total, back, 1)
     center, scale = moments(total, square, stats[2])
@@ -354,32 +381,40 @@
 
 
 def final_pass(
-    buf, late, tail, whole, from_ref, inverse, stats, level, level4,
+    edge, low, high, late, tail, whole, from_ref, inverse, centers, scales, level, level4,
     out, rolled, stage, sems,
 ):
     fields, rows, assets = out.shape
     main = rows // GROUP - SKIP_GROUPS
     first = LANE - 2 * fields * LATE_GROUPS
-    width = 2 * LANE
     late_tiles = (level[0], level[1], level4[0], level4[1])
-    main_tiles = (stats[0], stats[1], level[0], level[1])
     copies = []
+    half = main // 2
     for f in range(fields):
         for g in range(LATE_GROUPS):
             spot = first + f * LATE_GROUPS + g
-            cols = [column(t, spot, width) for t in late_tiles]
+            column_set = [column(t, spot, LANE) for t in late_tiles]
             where = rows_of(LATE_GROUPS + g)
-            final_rows(f, where, late, rows_of(g), inverse, stage, rows_of(g), cols, assets)
-        for g in range(main):
-            cols = [column(t, f * main + g, width) for t in main_tiles]
-            where = rows_of(g + SKIP_GROUPS)
-            put = rows_of(LATE_GROUPS + g)
-            final_rows(f, where, buf, where, inverse, stage, put, cols, assets)
-        copy = pltpu.make_async_copy(
-            stage.at[f], out.at[f, pl.ds(LATE, rows - LATE), :], sems.at[f]
-        )
-        copy.start()
-        copies.append(copy)
+            final_rows(f, where, late, rows_of(g), inverse, stage, rows_of(g), column_set)
+        for part in range(2):
+            for g in range(part * half, (part + 1) * half):
+                spot = f * main + g
+                c2, s2 = column(level[0], spot, LANE), column(level[1], spot, LANE)
+                where = rows_of(g + SKIP_GROUPS)
+                put = rows_of(g + LATE_GROUPS)
+                column_set = (centers[spot], scales[spot], c2, s2)
+                source = (low, high)[part]
+                mine = rows_of(g - part * half)
+                final_rows(f, where, source, mine, inverse, stage, put, column_set)
+            begin = part * (LATE_GROUPS + half) * GROUP
+            size = (half + (LATE_GROUPS if part == 0 else 0)) * GROUP
+            copy = pltpu.make_async_copy(
+                stage.at[f, pl.ds(begin, size), :],
+                out.at[f, pl.ds(LATE + begin, size), :],
+                sems.at[2 * f + part],
+            )
+            copy.start()
+            copies.append(copy)
     base = block_starts(rows)[0]
     width = 4 * LANE
     sub = sublanes(width)
@@ -395,7 +430,7 @@
             running, last = prefix_groups(masked, width)
             last = last + whole[f, :, lanes]
             for g in range(LATE_GROUPS):
-                r = buf[f, rows_of(g), lanes] + (last - running[g])
+                r = edge[f, rows_of(g), lanes] + (last - running[g])
                 rolled[f, rows_of(g), lanes] = r * inverse[rows_of(g), lanes]
             return carry
 
@@ -406,14 +441,13 @@
 
 def head_final_pass(rolled, inverse, sent, prior, out, stage, sems):
     fields, _, assets = rolled.shape
-    width = 2 * LANE
     levels = sent[...]
     copies = []
     for f in range(fields):
         for g in range(LATE_GROUPS):
-            cols = [column(levels, 16 * i + f * LATE_GROUPS + g, width) for i in range(4)]
+            cols = [column(levels, 16 * i + f * LATE_GROUPS + g, LANE) for i in range(4)]
             rows = rows_of(g)
-            final_rows(f, rows, rolled, rows, inverse, stage, rows, cols, assets)
+            final_rows(f, rows, rolled, rows, inverse, stage, rows, cols)
         copy = pltpu.make_async_copy(stage.at[f], out.at[f, pl.ds(0, LATE), :], sems.at[f])
         copy.start()
         copies.append(copy)
@@ -449,7 +483,7 @@
     slab = shape(fields, LATE, assets)
     near, head = call(
         cut, "cut", [HBM], (slab, slab), (VMEM, VMEM), [pltpu.SemaphoreType.DMA((2,))],
-        limit=50,
+        limit=44,
     )(values)
     tail_near = lax.ppermute(near, "tm", ring)
     head = lax.ppermute(head, "tm", back)
@@ -461,38 +495,43 @@
         lax.all_to_all, axis_name="asset", split_axis=0, concat_axis=0, tiled=True
     )
 
-    held, inverse, tally = call(
-        load, "load", [HBM] * 3,
-        (shape(fields, rows, assets), shape(rows + LATE, assets), shape(2 * GROUP, LANE)),
-        (VMEM,) * 3,
+    width = 2 * LANE
+    chunks = assets // width
+    half = shape(fields, (rows - WINDOW) // 2, assets)
+    edge, low, high, inverse, pay, far = call(
+        first_pass, "first_pass", [HBM] * 3,
+        (
+            shape(fields, WINDOW + LATE, assets), half, half,
+            shape(rows + LATE, assets), shape(n, 2 * GROUP, LANE), slab,
+        ),
+        (VMEM,) * 6,
         [
             pltpu.VMEM((1, assets), jnp.int32),
             pltpu.VMEM((1, assets), jnp.int32),
-            pltpu.SemaphoreType.DMA((3,)),
+            pltpu.VMEM((chunks, fields, rows, width), jnp.float32),
+            pltpu.VMEM((2, fields, main, GROUP, LANE), jnp.float32),
+            pltpu.SemaphoreType.DMA((chunks,)),
+            pltpu.SemaphoreType.DMA((2,)),
         ],
-        limit=40, flops=work,
+        limit=40, flops=20 * work,
     )(values, opened, closed)
-    buf, pay, far = call(
-        first_pass, "first_pass", [VMEM] * 4,
-        (shape(fields, rows + LATE, assets), shape(n, 2 * GROUP, LANE), slab),
-        (VMEM,) * 3,
-        [pltpu.VMEM((2, fields, main, GROUP, LANE), jnp.float32)], flops=20 * work,
-    )(held, opened, inverse, tally)
     tail_far = lax.ppermute(far, "tm", ring)
     gathered = exchange(pay)
-    stats, part = call(
-        second_pass, "second_pass", [VMEM] * 3,
-        (shape(3, GROUP, LANE), shape(2 * GROUP, LANE)), (VMEM, VMEM), limit=16, flops=10 * work,
-    )(gathered, buf, inverse)
+    columns = shape(fields * main, GROUP, LANE)
+    stats, part, centers, scales = call(
+        second_pass, "second_pass", [VMEM] * 4,
+        (shape(3, GROUP, LANE), shape(2 * GROUP, LANE), columns, columns), (VMEM,) * 4,
+        [pltpu.VMEM((2, fields * main, GROUP, LANE), jnp.float32)], limit=16, flops=10 * work,
+    )(gathered, low, high, inverse)
     late, whole, pay = call(
         late_first_pass, "late_first_pass", [VMEM] * 6,
         (shape(fields, 2 * LATE, assets), shape(fields, GROUP, assets), shape(n, 2 * GROUP, LANE)),
         (VMEM, VMEM, VMEM), limit=20, flops=5 * work,
-    )(buf, tail_near, head, opened, inverse, part)
+    )(edge, tail_near, head, opened, inverse, part)
     gathered = exchange(pay)
     level, pay = call(
         late_second_pass, "late_second_pass", [VMEM] * 4,
-        (pair, shape(n, GROUP, LANE)), (VMEM, VMEM), limit=16, flops=3 * work,
+        (pair, shape(n, GROUP // 2, LANE)), (VMEM, VMEM), limit=16, flops=3 * work,
     )(gathered, stats, late, inverse)
     gathered = exchange(pay)
     level4, pay = call(
@@ -500,14 +539,14 @@
     )(gathered, stats, level)
     sent = lax.ppermute(pay, "tm", ring)
     out, rolled = call(
-        final_pass, "final_pass", [VMEM] * 9,
+        final_pass, "final_pass", [VMEM] * 12,
         (shape(fields, rows, assets), slab), (HBM, VMEM),
         [
             pltpu.VMEM((fields, rows - LATE, assets), jnp.float32),
-            pltpu.SemaphoreType.DMA((fields,)),
+            pltpu.SemaphoreType.DMA((2 * fields,)),
         ],
         limit=16, flops=10 * work,
-    )(buf, late, tail_far, whole, opened, inverse, stats, level, level4)
+    )(edge, low, high, late, tail_far, whole, opened, inverse, centers, scales, level, level4)
     return call(
         head_final_pass, "head_final_pass", [VMEM] * 3 + [HBM],
         shape(fields, rows, assets), HBM,

time: 68.4 us -> 66.4 us (0.971)
  Pallas kernels: 21.2 us -> 18.4 us
  blocking collectives: 41.9 us -> 43.6 us
  starting transfers between devices: 4.88 us -> 3.72 us
    pallas_call x4 -> x3, Pallas kernels: 15.5 us -> 12.6 us  [the longest x1 6.75 us: per_device(): call(first_pass, 'first_pass', [HBM] * 3, (shape(fields, WINDOW + LATE, a...]
    all_to_all x3, blocking collectives: 41.9 us -> 43.6 us  [per_device(): gathered = exchange(pay)]
    ppermute x1, starting transfers between devices: 1.25 us -> 0.09 us  [per_device(): sent = lax.ppermute(pay, 'tm', ring)]
  transfers between devices with their start and end apart: 4 -> 4, of which waited for: 0 -> 1; matrix products, arithmetic and copies ran while one was open for 0% -> 0% of each run, Pallas kernels for 27% -> 24%
where the time goes in v4:
time: 66.4 us; the launch traced here: 66 us
  blocking collectives  43.6 us (66%)
  Pallas kernels  18.4 us (28%)
  starting transfers between devices  3.72 us (6%)
    all_to_all x3, blocking collectives, per_device(): gathered = exchange(pay)  43.6 us
    pallas_call x1, Pallas kernels, per_device(): call(first_pass, 'first_pass', [HBM] * 3, (shape(fields, WINDOW + LATE, a...  6.75 us
    pallas_call x1, Pallas kernels, per_device(): call(final_pass, 'final_pass', [VMEM] * 12, (shape(fields, rows, assets),...  3.36 us
    pallas_call x1, Pallas kernels, per_device(): call(second_pass, 'second_pass', [VMEM] * 4, (shape(3, GROUP, LANE), shap...  2.5 us
    ppermute x1, starting transfers between devices, per_device(): tail_near = lax.ppermute(near, 'tm', ring)  2.1 us
    pallas_call x1, Pallas kernels, per_device(): call(late_first_pass, 'late_first_pass', [VMEM] * 6, (shape(fields, 2 * L...  1.83 us
    pallas_call x1, Pallas kernels, per_device(): call(cut, 'cut', [HBM], (slab, slab), (VMEM, VMEM), [pltpu.SemaphoreType....  1.58 us
    ppermute x1, starting transfers between devices, per_device(): head = lax.ppermute(head, 'tm', back)  1.35 us
  transfers between devices with their start and end apart: 4, of which 1 were waited for; matrix products, arithmetic and copies ran while one was open for 0% of the time, Pallas kernels for 24%

profile of v4, /device:TPU:1, one launch (start us, length us, event | category | flops | bytes accessed | tf_op | source)
XLA Modules:
  0.0 66.0 jit_solution(16281954885869294098)
XLA Ops:
  0.0 0.0 copy-start.1
  0.0 0.0 copy-start
  0.0 1.6 %cut.1 = (f32[4,32,2048]{2,1,0:T(8,128)S(1)}, f32[4,32,2048]{2,1,0:T(8,128)S(1)}) custom-call(f32[4,256,2048]{2,1,0:T(8,128)} %x_hbm.3), custom_call_target="tpu_custom_call" | custom-call | tf_op jit(solution)/shard_map/cut/pallas_call | solution.py:484
  1.6 2.1 %collective-permute-start = (f32[4,32,2048]{2,1,0:T(8,128)S(1)}, f32[4,32,2048]{2,1,0:T(8,128)S(1)}, u32[]{:S(2)}, u32[]{:S(2)}) collective-permute-start(f32[4,32,2048]{2,1,0:T(8,128)S(1)} %get-tuple-element.29), channel_id=1, source_target_pairs={{0,1},{1,2},{2,3},{3,0},{4,5},{5,6},{6,7},{7,4},{8,9},{9,10},{10,1... | collective-permute-start | bytes 3145736 | tf_op jit(solution)/shard_map/ppermute | solution.py:488
  3.7 1.3 %collective-permute-start.1 = (f32[4,32,2048]{2,1,0:T(8,128)S(1)}, f32[4,32,2048]{2,1,0:T(8,128)S(1)}, u32[]{:S(2)}, u32[]{:S(2)}) collective-permute-start(f32[4,32,2048]{2,1,0:T(8,128)S(1)} %get-tuple-element.30), channel_id=1, source_target_pairs={{1,0},{2,1},{3,2},{0,3},{5,4},{6,5},{7,6},{4,7},{9,8},{10,9},{11,1... | collective-permute-start | bytes 3145736 | tf_op jit(solution)/shard_map/ppermute | solution.py:489
  5.0 0.0 copy-done.1
  5.0 0.0 copy-done
  5.0 6.7 %first_pass.1 = (f32[4,96,2048]{2,1,0:T(8,128)S(1)}, f32[4,96,2048]{2,1,0:T(8,128)S(1)}, f32[4,96,2048]{2,1,0:T(8,128)S(1)}, f32[288,2048]{1,0:T(8,128)S(1)}, f3...) custom-call(f32[4,256,2048]{2,1,0:T(8,128)} %x_hbm.3, s32[1,2048]{1,0:T(1,128)S(1)} %bitcast.2, s32[1,2048]{1,0:T(1,128)S(1)} %bitcast.5), custom_call_target="tpu_custom_call" | custom-call | flops 41943040 | tf_op jit(solution)/shard_map/first_pass/pallas_call | solution.py:501
  11.8 0.2 collective-permute-start.2
  12.0 18.4 %all_to_all.15.gathered = f32[32,16,128]{2,1,0:T(8,128)S(1)} all-to-all(f32[32,16,128]{2,1,0:T(8,128)S(1)} %get-tuple-element.32), channel_id=1, replica_groups=mesh['asset'=32,'tm'=4] {'asset'}, dimensions={0} | all-to-all | bytes 524288 | tf_op jit(solution)/shard_map/all_to_all | solution.py:519
  30.4 2.5 %second_pass.1 = (f32[3,8,128]{2,1,0:T(8,128)S(1)}, f32[16,128]{1,0:T(8,128)S(1)}, f32[96,8,128]{2,1,0:T(8,128)S(1)}, f32[96,8,128]{2,1,0:T(8,128)S(1)}) custom-call(f32[32,16,128]{2,1,0:T(8,128)S(1)} %all_to_all.15.gathered, f32[4,96,2048]{2,1,0:T(8,128)S(1)} %get-tuple-element.27.low, f32[4,96,2048]{2,1,0:T(8,128)S(1)} %get-tuple-element.28.high, ...), custom_call_target="tpu_custom_call" | custom-call | flops 20971520 | tf_op jit(solution)/shard_map/second_pass/pallas_call | solution.py:521
  32.9 0.0 collective-permute-done.tail
  32.9 0.0 collective-permute-done.1.head
  32.9 1.8 %late_first_pass.1 = (f32[4,64,2048]{2,1,0:T(8,128)S(1)}, f32[4,8,2048]{2,1,0:T(8,128)S(1)}, f32[32,16,128]{2,1,0:T(8,128)S(1)}) custom-call(f32[4,96,2048]{2,1,0:T(8,128)S(1)} %get-tuple-element.26.edge, f32[4,32,2048]{2,1,0:T(8,128)S(1)} %collective-permute-done.tail, f32[4,32,2048]{2,1,0:T(8,128)S(1)} %collective-permute-done.1.head, ...), custom_call_target="tpu_custom_call" | custom-call | flops 10485760 | tf_op jit(solution)/shard_map/late_first_pass/pallas_call | solution.py:526
  34.7 14.4 %all_to_all.16.gathered = f32[32,16,128]{2,1,0:T(8,128)S(1)} all-to-all(f32[32,16,128]{2,1,0:T(8,128)S(1)} %get-tuple-element.39), channel_id=1, replica_groups=mesh['asset'=32,'tm'=4] {'asset'}, dimensions={0} | all-to-all | bytes 524288 | tf_op jit(solution)/shard_map/all_to_all | solution.py:531
  49.1 1.0 %late_second_pass.1 = (f32[2,8,128]{2,1,0:T(8,128)S(1)}, f32[32,4,128]{2,1,0:T(4,128)S(1)}) custom-call(f32[32,16,128]{2,1,0:T(8,128)S(1)} %all_to_all.16.gathered, f32[3,8,128]{2,1,0:T(8,128)S(1)} %get-tuple-element.40.stats, f32[4,64,2048]{2,1,0:T(8,128)S(1)} %get-tuple-element.34.late, f32[288,2048]{1,0:T(8,128)S(1)} %get-tuple-element.31.inverse), custom_call_target="tpu_custom_call" | custom-call | flops 6291456 | tf_op jit(solution)/shard_map/late_second_pass/pallas_call | solution.py:532
  50.1 10.8 %all_to_all.17.gathered = f32[32,4,128]{2,1,0:T(4,128)S(1)} all-to-all(f32[32,4,128]{2,1,0:T(4,128)S(1)} %get-tuple-element.42), channel_id=1, replica_groups=mesh['asset'=32,'tm'=4] {'asset'}, dimensions={0} | all-to-all | bytes 131072 | tf_op jit(solution)/shard_map/all_to_all | solution.py:536
  60.9 0.2 send_pass.1
  61.1 0.1 collective-permute-start.3
  61.2 0.0 collective-permute-done.2.tail
  61.2 3.4 %final_pass.1 = (f32[4,256,2048]{2,1,0:T(8,128)}, f32[4,32,2048]{2,1,0:T(8,128)S(1)}) custom-call(f32[4,96,2048]{2,1,0:T(8,128)S(1)} %get-tuple-element.26.edge, f32[4,96,2048]{2,1,0:T(8,128)S(1)} %get-tuple-element.27.low, f32[4,96,2048]{2,1,0:T(8,128)S(1)} %get-tuple-element.28.high, f32[4,64,2048]{2,1,0:T(8,128)S(1)} %get-tuple-element.34.late, ...), custom_call_target="tpu_custom_call" | custom-call | flops 20971520 | tf_op jit(solution)/shard_map/final_pass/pallas_call | solution.py:541
  64.6 0.2 collective-permute-done.3.sent
  64.8 1.1 %head_final_pass.1 = f32[4,256,2048]{2,1,0:T(8,128)} custom-call(f32[4,32,2048]{2,1,0:T(8,128)S(1)} %get-tuple-element.44.rolled, f32[288,2048]{1,0:T(8,128)S(1)} %get-tuple-element.31.inverse, f32[8,128]{1,0:T(8,128)S(1)} %collective-permute-done.3.sent, f32[4,256,2048]{2,1,0:T(8,128)} %get-tuple-element.46.prior), custom_call_target="tpu_custom_call", output_to_operand_aliasing={{}: (3, {})} | custom-call | flops 4194304 | tf_op jit(solution)/shard_map/head_final_pass/pallas_call | solution.py:550
Async XLA Ops:
  0.0 5.0 %copy-start.1 = (s32[2048]{0:T(1024)S(1)}, s32[2048]{0:T(1024)}, u32[]{:S(2)}) copy-start(s32[2048]{0:T(1024)} %param.5) | copy-start | bytes 24580
  0.0 5.0 %copy-start = (s32[2048]{0:T(1024)S(1)}, s32[2048]{0:T(1024)}, u32[]{:S(2)}) copy-start(s32[2048]{0:T(1024)} %param.4) | copy-start | bytes 24580
  1.6 31.3 %collective-permute-start = (f32[4,32,2048]{2,1,0:T(8,128)S(1)}, f32[4,32,2048]{2,1,0:T(8,128)S(1)}, u32[]{:S(2)}, u32[]{:S(2)}) collective-permute-start(f32[4,32,2048]{2,1,0:T(8,128)S(1)} %get-tuple-element.29), channel_id=1, source_target_pairs={{0,1},{1,2},{2,3},{3,0},{4,5},{5,6},{6,7},{7,4},{8,9},{9,10},{10,1... | collective-permute-start | bytes 3145736 | tf_op jit(solution)/shard_map/ppermute | solution.py:488
  3.7 29.2 %collective-permute-start.1 = (f32[4,32,2048]{2,1,0:T(8,128)S(1)}, f32[4,32,2048]{2,1,0:T(8,128)S(1)}, u32[]{:S(2)}, u32[]{:S(2)}) collective-permute-start(f32[4,32,2048]{2,1,0:T(8,128)S(1)} %get-tuple-element.30), channel_id=1, source_target_pairs={{1,0},{2,1},{3,2},{0,3},{5,4},{6,5},{7,6},{4,7},{9,8},{10,9},{11,1... | collective-permute-start | bytes 3145736 | tf_op jit(solution)/shard_map/ppermute | solution.py:489
  11.8 49.4 %collective-permute-start.2 = (f32[4,32,2048]{2,1,0:T(8,128)S(1)}, f32[4,32,2048]{2,1,0:T(8,128)S(1)}, u32[]{:S(2)}, u32[]{:S(2)}) collective-permute-start(f32[4,32,2048]{2,1,0:T(8,128)S(1)} %get-tuple-element.35), channel_id=1, source_target_pairs={{0,1},{1,2},{2,3},{3,0},{4,5},{5,6},{6,7},{7,4},{8,9},{9,10},{10,1... | collective-permute-start | bytes 3145736 | tf_op jit(solution)/shard_map/ppermute | solution.py:518
  61.1 3.7 %collective-permute-start.3 = (f32[8,128]{1,0:T(8,128)S(1)}, f32[8,128]{1,0:T(8,128)S(1)}, u32[]{:S(2)}, u32[]{:S(2)}) collective-permute-start(f32[8,128]{1,0:T(8,128)S(1)} %get-tuple-element.45), channel_id=1, source_target_pairs={{0,1},{1,2},{2,3},{3,0},{4,5},{5,6},{6,7},{7,4},{8,9},{9,10},{10,1... | collective-permute-start | bytes 12296 | tf_op jit(solution)/shard_map/ppermute | solution.py:540

commit v5 on v4

--- a/solution.py
+++ b/solution.py
@@ -515,7 +515,6 @@
         ],
         limit=40, flops=20 * work,
     )(values, opened, closed)
-    tail_far = lax.ppermute(far, "tm", ring)
     gathered = exchange(pay)
     columns = shape(fields * main, GROUP, LANE)
     stats, part, centers, scales = call(
@@ -523,6 +522,8 @@
         (shape(3, GROUP, LANE), shape(2 * GROUP, LANE), columns, columns), (VMEM,) * 4,
         [pltpu.VMEM((2, fields * main, GROUP, LANE), jnp.float32)], limit=16, flops=10 * work,
     )(gathered, low, high, inverse)
+    far, part = lax.optimization_barrier((far, part))
+    tail_far = lax.ppermute(far, "tm", ring)
     late, whole, pay = call(
         late_first_pass, "late_first_pass", [VMEM] * 6,
         (shape(fields, 2 * LATE, assets), shape(fields, GROUP, assets), shape(n, 2 * GROUP, LANE)),

time: 66.4 us -> 66 us (level)
  blocking collectives: 43.6 us -> 42.5 us
  starting transfers between devices: 3.72 us -> 4.74 us
    ppermute x1, starting transfers between devices: 0.09 us -> 1.22 us  [per_device(): sent = lax.ppermute(pay, 'tm', ring)]
    all_to_all x3, blocking collectives: 43.6 us -> 42.5 us  [per_device(): gathered = exchange(pay)]
  transfers between devices with their start and end apart: 4 -> 4, of which waited for: 1 -> 0; matrix products, arithmetic and copies ran while one was open for 0% -> 0% of each run, Pallas kernels for 24% -> 24%
where the time goes in v5:
time: 66 us; the launch traced here: 65.8 us
  blocking collectives  42.5 us (64%)
  Pallas kernels  18.4 us (28%)
  starting transfers between devices  4.74 us (7%)
    all_to_all x3, blocking collectives, per_device(): gathered = exchange(pay)  42.5 us
    pallas_call x1, Pallas kernels, per_device(): call(first_pass, 'first_pass', [HBM] * 3, (shape(fields, WINDOW + LATE, a...  6.75 us
    pallas_call x1, Pallas kernels, per_device(): call(final_pass, 'final_pass', [VMEM] * 12, (shape(fields, rows, assets),...  3.36 us
    pallas_call x1, Pallas kernels, per_device(): call(second_pass, 'second_pass', [VMEM] * 4, (shape(3, GROUP, LANE), shap...  2.5 us
    ppermute x1, starting transfers between devices, per_device(): tail_near = lax.ppermute(near, 'tm', ring)  2.1 us
    pallas_call x1, Pallas kernels, per_device(): call(late_first_pass, 'late_first_pass', [VMEM] * 6, (shape(fields, 2 * L...  1.83 us
    pallas_call x1, Pallas kernels, per_device(): call(cut, 'cut', [HBM], (slab, slab), (VMEM, VMEM), [pltpu.SemaphoreType....  1.58 us
    ppermute x1, starting transfers between devices, per_device(): head = lax.ppermute(head, 'tm', back)  1.35 us
  transfers between devices with their start and end apart: 4, of which 0 were waited for; matrix products, arithmetic and copies ran while one was open for 0% of the time, Pallas kernels for 24%

profile of v5, /device:TPU:1, one launch (start us, length us, event | category | flops | bytes accessed | tf_op | source)
XLA Modules:
  0.0 65.8 jit_solution(11053350099155878393)
XLA Ops:
  0.0 0.0 copy-start.1
  0.0 0.0 copy-start
  0.0 1.6 %cut.1 = (f32[4,32,2048]{2,1,0:T(8,128)S(1)}, f32[4,32,2048]{2,1,0:T(8,128)S(1)}) custom-call(f32[4,256,2048]{2,1,0:T(8,128)} %x_hbm.3), custom_call_target="tpu_custom_call" | custom-call | tf_op jit(solution)/shard_map/cut/pallas_call | solution.py:484
  1.6 2.1 %collective-permute-start = (f32[4,32,2048]{2,1,0:T(8,128)S(1)}, f32[4,32,2048]{2,1,0:T(8,128)S(1)}, u32[]{:S(2)}, u32[]{:S(2)}) collective-permute-start(f32[4,32,2048]{2,1,0:T(8,128)S(1)} %get-tuple-element.31), channel_id=1, source_target_pairs={{0,1},{1,2},{2,3},{3,0},{4,5},{5,6},{6,7},{7,4},{8,9},{9,10},{10,1... | collective-permute-start | bytes 3145736 | tf_op jit(solution)/shard_map/ppermute | solution.py:488
  3.7 1.3 %collective-permute-start.1 = (f32[4,32,2048]{2,1,0:T(8,128)S(1)}, f32[4,32,2048]{2,1,0:T(8,128)S(1)}, u32[]{:S(2)}, u32[]{:S(2)}) collective-permute-start(f32[4,32,2048]{2,1,0:T(8,128)S(1)} %get-tuple-element.32), channel_id=1, source_target_pairs={{1,0},{2,1},{3,2},{0,3},{5,4},{6,5},{7,6},{4,7},{9,8},{10,9},{11,1... | collective-permute-start | bytes 3145736 | tf_op jit(solution)/shard_map/ppermute | solution.py:489
  5.0 0.0 copy-done.1
  5.0 0.0 copy-done
  5.0 6.7 %first_pass.1 = (f32[4,96,2048]{2,1,0:T(8,128)S(1)}, f32[4,96,2048]{2,1,0:T(8,128)S(1)}, f32[4,96,2048]{2,1,0:T(8,128)S(1)}, f32[288,2048]{1,0:T(8,128)S(1)}, f3...) custom-call(f32[4,256,2048]{2,1,0:T(8,128)} %x_hbm.3, s32[1,2048]{1,0:T(1,128)S(1)} %bitcast.2, s32[1,2048]{1,0:T(1,128)S(1)} %bitcast.5), custom_call_target="tpu_custom_call" | custom-call | flops 41943040 | tf_op jit(solution)/shard_map/first_pass/pallas_call | solution.py:501
  11.8 18.2 %all_to_all.15.gathered = f32[32,16,128]{2,1,0:T(8,128)S(1)} all-to-all(f32[32,16,128]{2,1,0:T(8,128)S(1)} %get-tuple-element.35), channel_id=1, replica_groups=mesh['asset'=32,'tm'=4] {'asset'}, dimensions={0} | all-to-all | bytes 524288 | tf_op jit(solution)/shard_map/all_to_all | solution.py:518
  30.0 2.5 %second_pass.1 = (f32[3,8,128]{2,1,0:T(8,128)S(1)}, f32[16,128]{1,0:T(8,128)S(1)}, f32[96,8,128]{2,1,0:T(8,128)S(1)}, f32[96,8,128]{2,1,0:T(8,128)S(1)}) custom-call(f32[32,16,128]{2,1,0:T(8,128)S(1)} %all_to_all.15.gathered, f32[4,96,2048]{2,1,0:T(8,128)S(1)} %get-tuple-element.29.low, f32[4,96,2048]{2,1,0:T(8,128)S(1)} %get-tuple-element.30.high, ...), custom_call_target="tpu_custom_call" | custom-call | flops 20971520 | tf_op jit(solution)/shard_map/second_pass/pallas_call | solution.py:520
  32.5 0.1 collective-permute-start.2
  32.6 0.0 collective-permute-done.tail
  32.6 0.0 collective-permute-done.1.head
  32.6 1.8 %late_first_pass.1 = (f32[4,64,2048]{2,1,0:T(8,128)S(1)}, f32[4,8,2048]{2,1,0:T(8,128)S(1)}, f32[32,16,128]{2,1,0:T(8,128)S(1)}) custom-call(f32[4,96,2048]{2,1,0:T(8,128)S(1)} %get-tuple-element.28.edge, f32[4,32,2048]{2,1,0:T(8,128)S(1)} %collective-permute-done.tail, f32[4,32,2048]{2,1,0:T(8,128)S(1)} %collective-permute-done.1.head, ...), custom_call_target="tpu_custom_call" | custom-call | flops 10485760 | tf_op jit(solution)/shard_map/late_first_pass/pallas_call | solution.py:527
  34.5 13.5 %all_to_all.16.gathered = f32[32,16,128]{2,1,0:T(8,128)S(1)} all-to-all(f32[32,16,128]{2,1,0:T(8,128)S(1)} %get-tuple-element.43), channel_id=1, replica_groups=mesh['asset'=32,'tm'=4] {'asset'}, dimensions={0} | all-to-all | bytes 524288 | tf_op jit(solution)/shard_map/all_to_all | solution.py:532
  48.0 1.0 %late_second_pass.1 = (f32[2,8,128]{2,1,0:T(8,128)S(1)}, f32[32,4,128]{2,1,0:T(4,128)S(1)}) custom-call(f32[32,16,128]{2,1,0:T(8,128)S(1)} %all_to_all.16.gathered, f32[3,8,128]{2,1,0:T(8,128)S(1)} %get-tuple-element.44.stats, f32[4,64,2048]{2,1,0:T(8,128)S(1)} %get-tuple-element.38.late, f32[288,2048]{1,0:T(8,128)S(1)} %get-tuple-element.33.inverse), custom_call_target="tpu_custom_call" | custom-call | flops 6291456 | tf_op jit(solution)/shard_map/late_second_pass/pallas_call | solution.py:533
  48.9 10.8 %all_to_all.17.gathered = f32[32,4,128]{2,1,0:T(4,128)S(1)} all-to-all(f32[32,4,128]{2,1,0:T(4,128)S(1)} %get-tuple-element.46), channel_id=1, replica_groups=mesh['asset'=32,'tm'=4] {'asset'}, dimensions={0} | all-to-all | bytes 131072 | tf_op jit(solution)/shard_map/all_to_all | solution.py:537
  59.8 0.2 send_pass.1
  60.0 1.2 %collective-permute-start.3 = (f32[8,128]{1,0:T(8,128)S(1)}, f32[8,128]{1,0:T(8,128)S(1)}, u32[]{:S(2)}, u32[]{:S(2)}) collective-permute-start(f32[8,128]{1,0:T(8,128)S(1)} %get-tuple-element.49), channel_id=1, source_target_pairs={{0,1},{1,2},{2,3},{3,0},{4,5},{5,6},{6,7},{7,4},{8,9},{9,10},{10,1... | collective-permute-start | bytes 12296 | tf_op jit(solution)/shard_map/ppermute | solution.py:541
  61.2 0.0 collective-permute-done.2.tail
  61.2 3.4 %final_pass.1 = (f32[4,256,2048]{2,1,0:T(8,128)}, f32[4,32,2048]{2,1,0:T(8,128)S(1)}) custom-call(f32[4,96,2048]{2,1,0:T(8,128)S(1)} %get-tuple-element.28.edge, f32[4,96,2048]{2,1,0:T(8,128)S(1)} %get-tuple-element.29.low, f32[4,96,2048]{2,1,0:T(8,128)S(1)} %get-tuple-element.30.high, f32[4,64,2048]{2,1,0:T(8,128)S(1)} %get-tuple-element.38.late, ...), custom_call_target="tpu_custom_call" | custom-call | flops 20971520 | tf_op jit(solution)/shard_map/final_pass/pallas_call | solution.py:542
  64.6 0.0 collective-permute-done.3.sent
  64.6 1.1 %head_final_pass.1 = f32[4,256,2048]{2,1,0:T(8,128)} custom-call(f32[4,32,2048]{2,1,0:T(8,128)S(1)} %get-tuple-element.48.rolled, f32[288,2048]{1,0:T(8,128)S(1)} %get-tuple-element.33.inverse, f32[8,128]{1,0:T(8,128)S(1)} %collective-permute-done.3.sent, f32[4,256,2048]{2,1,0:T(8,128)} %get-tuple-element.50.prior), custom_call_target="tpu_custom_call", output_to_operand_aliasing={{}: (3, {})} | custom-call | flops 4194304 | tf_op jit(solution)/shard_map/head_final_pass/pallas_call | solution.py:551
Async XLA Ops:
  0.0 5.0 %copy-start.1 = (s32[2048]{0:T(1024)S(1)}, s32[2048]{0:T(1024)}, u32[]{:S(2)}) copy-start(s32[2048]{0:T(1024)} %param.5) | copy-start | bytes 24580
  0.0 5.0 %copy-start = (s32[2048]{0:T(1024)S(1)}, s32[2048]{0:T(1024)}, u32[]{:S(2)}) copy-start(s32[2048]{0:T(1024)} %param.4) | copy-start | bytes 24580
  1.6 31.0 %collective-permute-start = (f32[4,32,2048]{2,1,0:T(8,128)S(1)}, f32[4,32,2048]{2,1,0:T(8,128)S(1)}, u32[]{:S(2)}, u32[]{:S(2)}) collective-permute-start(f32[4,32,2048]{2,1,0:T(8,128)S(1)} %get-tuple-element.31), channel_id=1, source_target_pairs={{0,1},{1,2},{2,3},{3,0},{4,5},{5,6},{6,7},{7,4},{8,9},{9,10},{10,1... | collective-permute-start | bytes 3145736 | tf_op jit(solution)/shard_map/ppermute | solution.py:488
  3.7 28.9 %collective-permute-start.1 = (f32[4,32,2048]{2,1,0:T(8,128)S(1)}, f32[4,32,2048]{2,1,0:T(8,128)S(1)}, u32[]{:S(2)}, u32[]{:S(2)}) collective-permute-start(f32[4,32,2048]{2,1,0:T(8,128)S(1)} %get-tuple-element.32), channel_id=1, source_target_pairs={{1,0},{2,1},{3,2},{0,3},{5,4},{6,5},{7,6},{4,7},{9,8},{10,9},{11,1... | collective-permute-start | bytes 3145736 | tf_op jit(solution)/shard_map/ppermute | solution.py:489
  32.5 28.7 %collective-permute-start.2 = (f32[4,32,2048]{2,1,0:T(8,128)S(1)}, f32[4,32,2048]{2,1,0:T(8,128)S(1)}, u32[]{:S(2)}, u32[]{:S(2)}) collective-permute-start(f32[4,32,2048]{2,1,0:T(8,128)S(1)} %get-tuple-element.39), channel_id=1, source_target_pairs={{0,1},{1,2},{2,3},{3,0},{4,5},{5,6},{6,7},{7,4},{8,9},{9,10},{10,1... | collective-permute-start | bytes 3145736 | tf_op jit(solution)/shard_map/ppermute | solution.py:526
  60.0 4.6 %collective-permute-start.3 = (f32[8,128]{1,0:T(8,128)S(1)}, f32[8,128]{1,0:T(8,128)S(1)}, u32[]{:S(2)}, u32[]{:S(2)}) collective-permute-start(f32[8,128]{1,0:T(8,128)S(1)} %get-tuple-element.49), channel_id=1, source_target_pairs={{0,1},{1,2},{2,3},{3,0},{4,5},{5,6},{6,7},{7,4},{8,9},{9,10},{10,1... | collective-permute-start | bytes 12296 | tf_op jit(solution)/shard_map/ppermute | solution.py:541

commit v6 on v5

--- a/solution.py
+++ b/solution.py
@@ -250,18 +250,19 @@
     half = main // 2
     for source, skip in ((low, 0), (high, half)):
 
-        def group(i, carry):
-            g = i + skip
-            cs = [centers[f * main + g] for f in range(fields)]
-            ss = [scales[f * main + g] for f in range(fields)]
-            where = group_rows(g + SKIP_GROUPS)
-            acc = row_moments(source, group_rows(i), inverse, where, cs, ss)
-            for stat in range(2):
-                for f in range(fields):
-                    sums[stat, f * main + g] = acc[stat * fields + f]
+        def group(pair, carry):
+            for i in (2 * pair, 2 * pair + 1):
+                g = i + skip
+                cs = [centers[f * main + g] for f in range(fields)]
+                ss = [scales[f * main + g] for f in range(fields)]
+                where = group_rows(g + SKIP_GROUPS)
+                acc = row_moments(source, group_rows(i), inverse, where, cs, ss)
+                for stat in range(2):
+                    for f in range(fields):
+                        sums[stat, f * main + g] = acc[stat * fields + f]
             return carry
 
-        lax.fori_loop(0, half, group, 0)
+        lax.fori_loop(0, half // 2, group, 0)
     for stat in range(2):
         tile = jnp.zeros((GROUP, LANE), jnp.float32)
         for spot in range(first):
@@ -269,7 +270,7 @@
         part[rows_of(stat), :] = tile
 
 
-def late_first_pass(edge, tail, head, from_ref, inverse, part, late, whole, pay):
+def late_first_pass(edge, tail, head, from_ref, inverse, part, late, whole, pay, sums):
     fields, _, assets = edge.shape
     rows = inverse.shape[0] - LATE
     base, base_next = block_starts(rows)
@@ -311,11 +312,14 @@
 
         zero = jnp.zeros((GROUP, LANE), jnp.float32)
         acc = lax.fori_loop(0, assets // width, tile, (zero,) * (4 * LATE_GROUPS))
+        for i in range(4 * LATE_GROUPS):
+            sums[f, i] = acc[i]
+    for f in range(fields):
         for side in range(2):
             for g in range(LATE_GROUPS):
                 spot = first + (side * fields + f) * LATE_GROUPS + g
                 for stat in range(2):
-                    value = total_of(acc[(stat * 2 + side) * LATE_GROUPS + g])
+                    value = total_of(sums[f, (stat * 2 + side) * LATE_GROUPS + g])
                     tiles[stat] = jnp.where(lane == spot, value, tiles[stat])
     for d in range(pay.shape[0]):
         pay[d, :GROUP, :] = tiles[0]
@@ -527,7 +531,8 @@
     late, whole, pay = call(
         late_first_pass, "late_first_pass", [VMEM] * 6,
         (shape(fields, 2 * LATE, assets), shape(fields, GROUP, assets), shape(n, 2 * GROUP, LANE)),
-        (VMEM, VMEM, VMEM), limit=20, flops=5 * work,
+        (VMEM, VMEM, VMEM),
+        [pltpu.VMEM((fields, 4 * LATE_GROUPS, GROUP, LANE), jnp.float32)], limit=20, flops=5 * work,
     )(edge, tail_near, head, opened, inverse, part)
     gathered = exchange(pay)
     level, pay = call(

time: 66 us -> 65.8 us (level)
  transfers between devices with their start and end apart: 4 -> 4, of which waited for: 0 -> 0; matrix products, arithmetic and copies ran while one was open for 0% -> 0% of each run, Pallas kernels for 24% -> 23%
where the time goes in v6:
time: 65.8 us; the launch traced here: 65.6 us
  blocking collectives  42.7 us (65%)
  Pallas kernels  18.1 us (28%)
  starting transfers between devices  4.74 us (7%)
    all_to_all x3, blocking collectives, per_device(): gathered = exchange(pay)  42.7 us
    pallas_call x1, Pallas kernels, per_device(): call(first_pass, 'first_pass', [HBM] * 3, (shape(fields, WINDOW + LATE, a...  6.75 us
    pallas_call x1, Pallas kernels, per_device(): call(final_pass, 'final_pass', [VMEM] * 12, (shape(fields, rows, assets),...  3.36 us
    pallas_call x1, Pallas kernels, per_device(): call(second_pass, 'second_pass', [VMEM] * 4, (shape(3, GROUP, LANE), shap...  2.35 us
    ppermute x1, starting transfers between devices, per_device(): tail_near = lax.ppermute(near, 'tm', ring)  2.1 us
    pallas_call x1, Pallas kernels, per_device(): call(late_first_pass, 'late_first_pass', [VMEM] * 6, (shape(fields, 2 * L...  1.67 us
    pallas_call x1, Pallas kernels, per_device(): call(cut, 'cut', [HBM], (slab, slab), (VMEM, VMEM), [pltpu.SemaphoreType....  1.58 us
    ppermute x1, starting transfers between devices, per_device(): head = lax.ppermute(head, 'tm', back)  1.35 us
  transfers between devices with their start and end apart: 4, of which 0 were waited for; matrix products, arithmetic and copies ran while one was open for 0% of the time, Pallas kernels for 23%

profile of v6, /device:TPU:1, one launch (start us, length us, event | category | flops | bytes accessed | tf_op | source)
XLA Modules:
  0.0 65.6 jit_solution(7716152270523592589)
XLA Ops:
  0.0 0.0 copy-start.1
  0.0 0.0 copy-start
  0.0 1.6 %cut.1 = (f32[4,32,2048]{2,1,0:T(8,128)S(1)}, f32[4,32,2048]{2,1,0:T(8,128)S(1)}) custom-call(f32[4,256,2048]{2,1,0:T(8,128)} %x_hbm.3), custom_call_target="tpu_custom_call" | custom-call | tf_op jit(solution)/shard_map/cut/pallas_call | solution.py:488
  1.6 2.1 %collective-permute-start = (f32[4,32,2048]{2,1,0:T(8,128)S(1)}, f32[4,32,2048]{2,1,0:T(8,128)S(1)}, u32[]{:S(2)}, u32[]{:S(2)}) collective-permute-start(f32[4,32,2048]{2,1,0:T(8,128)S(1)} %get-tuple-element.31), channel_id=1, source_target_pairs={{0,1},{1,2},{2,3},{3,0},{4,5},{5,6},{6,7},{7,4},{8,9},{9,10},{10,1... | collective-permute-start | bytes 3145736 | tf_op jit(solution)/shard_map/ppermute | solution.py:492
  3.7 1.3 %collective-permute-start.1 = (f32[4,32,2048]{2,1,0:T(8,128)S(1)}, f32[4,32,2048]{2,1,0:T(8,128)S(1)}, u32[]{:S(2)}, u32[]{:S(2)}) collective-permute-start(f32[4,32,2048]{2,1,0:T(8,128)S(1)} %get-tuple-element.32), channel_id=1, source_target_pairs={{1,0},{2,1},{3,2},{0,3},{5,4},{6,5},{7,6},{4,7},{9,8},{10,9},{11,1... | collective-permute-start | bytes 3145736 | tf_op jit(solution)/shard_map/ppermute | solution.py:493
  5.0 0.0 copy-done.1
  5.0 0.0 copy-done
  5.0 6.7 %first_pass.1 = (f32[4,96,2048]{2,1,0:T(8,128)S(1)}, f32[4,96,2048]{2,1,0:T(8,128)S(1)}, f32[4,96,2048]{2,1,0:T(8,128)S(1)}, f32[288,2048]{1,0:T(8,128)S(1)}, f3...) custom-call(f32[4,256,2048]{2,1,0:T(8,128)} %x_hbm.3, s32[1,2048]{1,0:T(1,128)S(1)} %bitcast.2, s32[1,2048]{1,0:T(1,128)S(1)} %bitcast.5), custom_call_target="tpu_custom_call" | custom-call | flops 41943040 | tf_op jit(solution)/shard_map/first_pass/pallas_call | solution.py:505
  11.8 18.2 %all_to_all.15.gathered = f32[32,16,128]{2,1,0:T(8,128)S(1)} all-to-all(f32[32,16,128]{2,1,0:T(8,128)S(1)} %get-tuple-element.35), channel_id=1, replica_groups=mesh['asset'=32,'tm'=4] {'asset'}, dimensions={0} | all-to-all | bytes 524288 | tf_op jit(solution)/shard_map/all_to_all | solution.py:522
  30.0 2.3 %second_pass.1 = (f32[3,8,128]{2,1,0:T(8,128)S(1)}, f32[16,128]{1,0:T(8,128)S(1)}, f32[96,8,128]{2,1,0:T(8,128)S(1)}, f32[96,8,128]{2,1,0:T(8,128)S(1)}) custom-call(f32[32,16,128]{2,1,0:T(8,128)S(1)} %all_to_all.15.gathered, f32[4,96,2048]{2,1,0:T(8,128)S(1)} %get-tuple-element.29.low, f32[4,96,2048]{2,1,0:T(8,128)S(1)} %get-tuple-element.30.high, ...), custom_call_target="tpu_custom_call" | custom-call | flops 20971520 | tf_op jit(solution)/shard_map/second_pass/pallas_call | solution.py:524
  32.4 0.1 collective-permute-start.2
  32.4 0.0 collective-permute-done.tail
  32.5 0.0 collective-permute-done.1.head
  32.5 1.7 %late_first_pass.1 = (f32[4,64,2048]{2,1,0:T(8,128)S(1)}, f32[4,8,2048]{2,1,0:T(8,128)S(1)}, f32[32,16,128]{2,1,0:T(8,128)S(1)}) custom-call(f32[4,96,2048]{2,1,0:T(8,128)S(1)} %get-tuple-element.28.edge, f32[4,32,2048]{2,1,0:T(8,128)S(1)} %collective-permute-done.tail, f32[4,32,2048]{2,1,0:T(8,128)S(1)} %collective-permute-done.1.head, ...), custom_call_target="tpu_custom_call" | custom-call | flops 10485760 | tf_op jit(solution)/shard_map/late_first_pass/pallas_call | solution.py:531
  34.1 13.6 %all_to_all.16.gathered = f32[32,16,128]{2,1,0:T(8,128)S(1)} all-to-all(f32[32,16,128]{2,1,0:T(8,128)S(1)} %get-tuple-element.43), channel_id=1, replica_groups=mesh['asset'=32,'tm'=4] {'asset'}, dimensions={0} | all-to-all | bytes 524288 | tf_op jit(solution)/shard_map/all_to_all | solution.py:537
  47.8 1.0 %late_second_pass.1 = (f32[2,8,128]{2,1,0:T(8,128)S(1)}, f32[32,4,128]{2,1,0:T(4,128)S(1)}) custom-call(f32[32,16,128]{2,1,0:T(8,128)S(1)} %all_to_all.16.gathered, f32[3,8,128]{2,1,0:T(8,128)S(1)} %get-tuple-element.44.stats, f32[4,64,2048]{2,1,0:T(8,128)S(1)} %get-tuple-element.38.late, f32[288,2048]{1,0:T(8,128)S(1)} %get-tuple-element.33.inverse), custom_call_target="tpu_custom_call" | custom-call | flops 6291456 | tf_op jit(solution)/shard_map/late_second_pass/pallas_call | solution.py:538
  48.8 10.8 %all_to_all.17.gathered = f32[32,4,128]{2,1,0:T(4,128)S(1)} all-to-all(f32[32,4,128]{2,1,0:T(4,128)S(1)} %get-tuple-element.46), channel_id=1, replica_groups=mesh['asset'=32,'tm'=4] {'asset'}, dimensions={0} | all-to-all | bytes 131072 | tf_op jit(solution)/shard_map/all_to_all | solution.py:542
  59.6 0.2 send_pass.1
  59.9 1.2 %collective-permute-start.3 = (f32[8,128]{1,0:T(8,128)S(1)}, f32[8,128]{1,0:T(8,128)S(1)}, u32[]{:S(2)}, u32[]{:S(2)}) collective-permute-start(f32[8,128]{1,0:T(8,128)S(1)} %get-tuple-element.49), channel_id=1, source_target_pairs={{0,1},{1,2},{2,3},{3,0},{4,5},{5,6},{6,7},{7,4},{8,9},{9,10},{10,1... | collective-permute-start | bytes 12296 | tf_op jit(solution)/shard_map/ppermute | solution.py:546
  61.1 0.0 collective-permute-done.2.tail
  61.1 3.4 %final_pass.1 = (f32[4,256,2048]{2,1,0:T(8,128)}, f32[4,32,2048]{2,1,0:T(8,128)S(1)}) custom-call(f32[4,96,2048]{2,1,0:T(8,128)S(1)} %get-tuple-element.28.edge, f32[4,96,2048]{2,1,0:T(8,128)S(1)} %get-tuple-element.29.low, f32[4,96,2048]{2,1,0:T(8,128)S(1)} %get-tuple-element.30.high, f32[4,64,2048]{2,1,0:T(8,128)S(1)} %get-tuple-element.38.late, ...), custom_call_target="tpu_custom_call" | custom-call | flops 20971520 | tf_op jit(solution)/shard_map/final_pass/pallas_call | solution.py:547
  64.4 0.0 collective-permute-done.3.sent
  64.5 1.1 %head_final_pass.1 = f32[4,256,2048]{2,1,0:T(8,128)} custom-call(f32[4,32,2048]{2,1,0:T(8,128)S(1)} %get-tuple-element.48.rolled, f32[288,2048]{1,0:T(8,128)S(1)} %get-tuple-element.33.inverse, f32[8,128]{1,0:T(8,128)S(1)} %collective-permute-done.3.sent, f32[4,256,2048]{2,1,0:T(8,128)} %get-tuple-element.50.prior), custom_call_target="tpu_custom_call", output_to_operand_aliasing={{}: (3, {})} | custom-call | flops 4194304 | tf_op jit(solution)/shard_map/head_final_pass/pallas_call | solution.py:556
Async XLA Ops:
  0.0 5.0 %copy-start.1 = (s32[2048]{0:T(1024)S(1)}, s32[2048]{0:T(1024)}, u32[]{:S(2)}) copy-start(s32[2048]{0:T(1024)} %param.5) | copy-start | bytes 24580
  0.0 5.0 %copy-start = (s32[2048]{0:T(1024)S(1)}, s32[2048]{0:T(1024)}, u32[]{:S(2)}) copy-start(s32[2048]{0:T(1024)} %param.4) | copy-start | bytes 24580
  1.6 30.9 %collective-permute-start = (f32[4,32,2048]{2,1,0:T(8,128)S(1)}, f32[4,32,2048]{2,1,0:T(8,128)S(1)}, u32[]{:S(2)}, u32[]{:S(2)}) collective-permute-start(f32[4,32,2048]{2,1,0:T(8,128)S(1)} %get-tuple-element.31), channel_id=1, source_target_pairs={{0,1},{1,2},{2,3},{3,0},{4,5},{5,6},{6,7},{7,4},{8,9},{9,10},{10,1... | collective-permute-start | bytes 3145736 | tf_op jit(solution)/shard_map/ppermute | solution.py:492
  3.7 28.8 %collective-permute-start.1 = (f32[4,32,2048]{2,1,0:T(8,128)S(1)}, f32[4,32,2048]{2,1,0:T(8,128)S(1)}, u32[]{:S(2)}, u32[]{:S(2)}) collective-permute-start(f32[4,32,2048]{2,1,0:T(8,128)S(1)} %get-tuple-element.32), channel_id=1, source_target_pairs={{1,0},{2,1},{3,2},{0,3},{5,4},{6,5},{7,6},{4,7},{9,8},{10,9},{11,1... | collective-permute-start | bytes 3145736 | tf_op jit(solution)/shard_map/ppermute | solution.py:493
  32.4 28.7 %collective-permute-start.2 = (f32[4,32,2048]{2,1,0:T(8,128)S(1)}, f32[4,32,2048]{2,1,0:T(8,128)S(1)}, u32[]{:S(2)}, u32[]{:S(2)}) collective-permute-start(f32[4,32,2048]{2,1,0:T(8,128)S(1)} %get-tuple-element.39), channel_id=1, source_target_pairs={{0,1},{1,2},{2,3},{3,0},{4,5},{5,6},{6,7},{7,4},{8,9},{9,10},{10,1... | collective-permute-start | bytes 3145736 | tf_op jit(solution)/shard_map/ppermute | solution.py:530
  59.9 4.6 %collective-permute-start.3 = (f32[8,128]{1,0:T(8,128)S(1)}, f32[8,128]{1,0:T(8,128)S(1)}, u32[]{:S(2)}, u32[]{:S(2)}) collective-permute-start(f32[8,128]{1,0:T(8,128)S(1)} %get-tuple-element.49), channel_id=1, source_target_pairs={{0,1},{1,2},{2,3},{3,0},{4,5},{5,6},{6,7},{7,4},{8,9},{9,10},{10,1... | collective-permute-start | bytes 12296 | tf_op jit(solution)/shard_map/ppermute | solution.py:546
